TPU v7x, 256 devices: a whole 4x4x8 slice. The times are simulated.
256 devices in a mesh: ctx: 64 (over z, y, core), head: 4 (over x).
Axes of the slice: x: 4, y: 4, z: 8, core: 2. Of those that a mesh axis runs over, the one named last changes fastest.
Arguments:
- queries: bfloat16 [16384, 4096], P(('ctx', 'head')), may hold values from -6.5 to 6.5
- keys: bfloat16 [16384, 2048], P(('ctx', 'head')), may hold values from -6.5 to 6.5
- values: bfloat16 [16384, 2048], P(('ctx', 'head')), may hold values from -6 to 6
- grad_out: bfloat16 [16384, 4096], P(('ctx', 'head')), may hold values from -6 to 6
- segments: int32 [16384], P('ctx'), may hold values from 0 to 7, never falling along the last dimension, each value on 1 to 4096 neighbouring positions
Outputs:
- attended: bfloat16 [16384, 4096], P(('ctx', 'head'))
- grad_queries: bfloat16 [16384, 4096], P(('ctx', 'head'))
- grad_keys: bfloat16 [16384, 2048], P(('ctx', 'head'))
- grad_values: bfloat16 [16384, 2048], P(('ctx', 'head'))
Inputs may be any that keep to these rules, and one draw needn't show every extreme that they name: `segments`: document numbers never fall along the sequence; each document holds 1 to 4096 tokens.
All inputs are finite; a program needn't handle non-finite values.
Results may differ from a plain program's by a relative error of at most 0.019.
Values may be sent and summed in bfloat16 or wider, within the bound.
A program may use at most 64 MiB of HBM per device.

v0:
```python
import jax
import jax.numpy as jnp
from jax import lax
from jax.sharding import PartitionSpec as P

QHEADS = 32
KVHEADS = 16
HEAD_DIM = 128
WINDOW = 1024


ATTN_SCALE = 168.0 ** (-0.5)


def from_behind(block, axis, distance):
    devices = range(lax.axis_size(axis))
    route = [(i - distance, i) for i in devices if i - distance in devices]
    return lax.ppermute(block, axis, route)


def shortened(value):
    return jax.tree.map(lambda a: a.astype(jnp.bfloat16) if a.dtype == jnp.float32 else a, value)


def visible_pairs(query_ids, key_ids, query_pos, key_pos, seq_total):
    distance = query_pos[:, None] - key_pos[None, :]
    inside = (distance >= 0) & (distance < WINDOW)
    present = (key_pos[None, :] >= 0) & (query_pos[:, None] < seq_total)
    return (query_ids[:, None] == key_ids[None, :]) & inside & present


def query_side(local_queries, local_grads, keys_all, values_all, visible):
    row_count = local_queries.shape[0]
    key_count = keys_all.shape[0]
    group_count = keys_all.shape[1] // HEAD_DIM
    per_group = QHEADS // KVHEADS
    query_width = per_group * HEAD_DIM
    key_start = jnp.zeros((key_count, group_count * HEAD_DIM), jnp.float32)
    stat_start = jnp.zeros((row_count, group_count * per_group), jnp.float32)
    initial = (
        jnp.zeros_like(local_queries),
        jnp.zeros_like(local_queries),
        stat_start,
        stat_start,
        key_start,
        key_start,
    )

    def one_group(group_index, carried):
        attended, grad_query, logsum, delta_all, grad_key, grad_value = carried
        column = group_index * query_width
        block_queries = lax.dynamic_slice_in_dim(local_queries, column, query_width, 1).reshape(
            row_count, per_group, HEAD_DIM
        )
        block_grads = lax.dynamic_slice_in_dim(local_grads, column, query_width, 1).reshape(
            row_count, per_group, HEAD_DIM
        )
        block_keys = lax.dynamic_slice_in_dim(keys_all, group_index * HEAD_DIM, HEAD_DIM, 1)
        block_values = lax.dynamic_slice_in_dim(values_all, group_index * HEAD_DIM, HEAD_DIM, 1)
        scores = (
            jnp.einsum("and,cd->nac", block_queries, block_keys, preferred_element_type=jnp.float32)
            * ATTN_SCALE
        )
        masked = jnp.where(visible[None], scores, -jnp.inf)
        highest = jnp.max(masked, axis=2, keepdims=True)
        weights = jnp.exp(masked - highest)
        totals = jnp.sum(weights, axis=2, keepdims=True)
        probs = weights / totals
        group_logsum = (highest + jnp.log(totals))[:, :, 0]
        probs_low = probs.astype(jnp.bfloat16)
        outputs = jnp.einsum(
            "nac,cd->and", probs_low, block_values, preferred_element_type=jnp.float32
        ).astype(jnp.bfloat16)
        group_delta = jnp.sum(outputs.astype(jnp.float32) * block_grads.astype(jnp.float32), axis=2)
        prob_grads = jnp.einsum(
            "and,cd->nac", block_grads, block_values, preferred_element_type=jnp.float32
        )
        score_grads = (ATTN_SCALE * probs * (prob_grads - group_delta.T[:, :, None])).astype(
            jnp.bfloat16
        )
        query_grads = jnp.einsum(
            "nac,cd->and", score_grads, block_keys, preferred_element_type=jnp.float32
        ).astype(jnp.bfloat16)
        attended = lax.dynamic_update_slice_in_dim(
            attended, outputs.reshape(row_count, query_width), column, 1
        )
        grad_query = lax.dynamic_update_slice_in_dim(
            grad_query, query_grads.reshape(row_count, query_width), column, 1
        )
        logsum = lax.dynamic_update_slice_in_dim(logsum, group_logsum.T, group_index * per_group, 1)
        delta_all = lax.dynamic_update_slice_in_dim(
            delta_all, group_delta, group_index * per_group, 1
        )
        key_part = jnp.einsum(
            "nac,and->cd", score_grads, block_queries, preferred_element_type=jnp.float32
        )
        value_part = jnp.einsum(
            "nac,and->cd", probs_low, block_grads, preferred_element_type=jnp.float32
        )
        grad_key = lax.dynamic_update_slice_in_dim(grad_key, key_part, group_index * HEAD_DIM, 1)
        grad_value = lax.dynamic_update_slice_in_dim(
            grad_value, value_part, group_index * HEAD_DIM, 1
        )
        return (attended, grad_query, logsum, delta_all, grad_key, grad_value)

    return lax.fori_loop(0, group_count, one_group, initial)


def body(queries, keys, values, grad_out, segments):
    local_queries, local_keys, local_values, local_grads = (
        lax.all_to_all(queries, "head", split_axis=1, concat_axis=0, tiled=True),
        lax.all_to_all(keys, "head", split_axis=1, concat_axis=0, tiled=True),
        lax.all_to_all(values, "head", split_axis=1, concat_axis=0, tiled=True),
        lax.all_to_all(grad_out, "head", split_axis=1, concat_axis=0, tiled=True),
    )
    row_count = local_queries.shape[0]
    reach_runs = WINDOW // row_count
    first_pos = lax.axis_index("ctx") * row_count
    seq_total = row_count * lax.axis_size("ctx")
    own_pos = first_pos + jnp.arange(row_count, dtype=jnp.int32)
    collected = from_behind((local_keys, local_values, segments), "ctx", 1)
    covered = 1
    while covered < reach_runs:
        further = from_behind((collected[0], collected[1], shortened(collected[2])), "ctx", covered)
        collected = tuple(
            (jnp.concatenate((older, newer), 0) for older, newer in zip(further, collected))
        )
        covered = covered * 2
    near_keys = collected[0]
    near_values = collected[1]
    near_ids = collected[2]
    keys_all = jnp.concatenate((near_keys, local_keys), 0)
    values_all = jnp.concatenate((near_values, local_values), 0)
    key_ids = jnp.concatenate((near_ids, segments), 0)
    key_pos = (
        first_pos
        - reach_runs * row_count
        + jnp.arange((reach_runs + 1) * row_count, dtype=jnp.int32)
    )
    visible = visible_pairs(segments, key_ids, own_pos, key_pos, seq_total)
    attended, grad_query, logsum, delta_all, grad_key, grad_value = query_side(
        local_queries, local_grads, keys_all, values_all, visible
    )
    key_total = grad_key[reach_runs * row_count :]
    value_total = grad_value[reach_runs * row_count :]
    for offset in range(1, reach_runs + 1):
        piece_start = (reach_runs - offset) * row_count
        key_piece = grad_key[piece_start : piece_start + row_count]
        value_piece = grad_value[piece_start : piece_start + row_count]
        back_keys, back_values = (
            from_behind(key_piece.astype(jnp.bfloat16), "ctx", -offset).astype(key_piece.dtype),
            from_behind(value_piece.astype(jnp.bfloat16), "ctx", -offset).astype(value_piece.dtype),
        )
        key_total = key_total + back_keys
        value_total = value_total + back_values
    grad_keys = key_total.astype(jnp.bfloat16)
    grad_values = value_total.astype(jnp.bfloat16)
    return (
        lax.all_to_all(attended, "head", split_axis=0, concat_axis=1, tiled=True),
        lax.all_to_all(grad_query, "head", split_axis=0, concat_axis=1, tiled=True),
        lax.all_to_all(grad_keys, "head", split_axis=0, concat_axis=1, tiled=True),
        lax.all_to_all(grad_values, "head", split_axis=0, concat_axis=1, tiled=True),
    )


def solution(mesh):
    return jax.shard_map(
        body,
        mesh=mesh,
        in_specs=(
            P(("ctx", "head"), None),
            P(("ctx", "head"), None),
            P(("ctx", "head"), None),
            P(("ctx", "head"), None),
            P("ctx"),
        ),
        out_specs=(
            P(("ctx", "head"), None),
            P(("ctx", "head"), None),
            P(("ctx", "head"), None),
            P(("ctx", "head"), None),
        ),
        check_vma=False,
    )
```

profile of v0, /device:TPU:120, one launch (start us, length us, event | category | flops | bytes accessed | tf_op | source)
XLA Modules:
  0.0 226.2 jit_solution(9701042405007195904)
XLA Ops:
  0.6 1.7 copy.152
  2.3 4.3 %all-to-all-start = ((bf16[64,4,512]{2,0,1:T(8,128)(2,1)}), bf16[64,4,512]{2,0,1:T(8,128)(2,1)S(1)}, u32[]{:S(2)}, u32[]{:S(2)}) async-start(bf16[64,4,512]{2,0,1:T(8,128)(2,1)} %bitcast.110), calls=%async_computation | async-start | bytes 524288 | tf_op jit(solution)/shard_map/all_to_all | solution.py:113
  6.6 1.7 copy.151
  8.3 4.9 %all-to-all-done = bf16[64,4,512]{2,0,1:T(8,128)(2,1)S(1)} async-done(((bf16[64,4,512]{2,0,1:T(8,128)(2,1)}), bf16[64,4,512]{2,0,1:T(8,128)(2,1)S(1)}, u32[]{:S(2)}, u32[]{:S(2)}) %all-to-all-start) | async-done | bytes 262176 | tf_op jit(solution)/shard_map/all_to_all | solution.py:113
  13.3 3.4 %all-to-all-start.1 = ((bf16[64,4,512]{2,0,1:T(8,128)(2,1)}), bf16[64,4,512]{2,0,1:T(8,128)(2,1)S(1)}, u32[]{:S(2)}, u32[]{:S(2)}) async-start(bf16[64,4,512]{2,0,1:T(8,128)(2,1)} %bitcast.109), calls=%async_computation.1 | async-start | bytes 524288 | tf_op jit(solution)/shard_map/all_to_all | solution.py:112
  16.7 1.9 collective-permute-start
  18.6 4.7 %all-to-all-done.1 = bf16[64,4,512]{2,0,1:T(8,128)(2,1)S(1)} async-done(((bf16[64,4,512]{2,0,1:T(8,128)(2,1)}), bf16[64,4,512]{2,0,1:T(8,128)(2,1)S(1)}, u32[]{:S(2)}, u32[]{:S(2)}) %all-to-all-start.1) | async-done | bytes 262176 | tf_op jit(solution)/shard_map/all_to_all | solution.py:112
  23.3 1.9 collective-permute-start.6
  25.3 4.8 %collective-permute-start.1 = (bf16[256,512]{1,0:T(8,128)(2,1)S(1)}, bf16[256,512]{1,0:T(8,128)(2,1)S(1)}, u32[]{:S(2)}, u32[]{:S(2)}) collective-permute-start(bf16[256,512]{1,0:T(8,128)(2,1)S(1)} %collective-permute-done), channel_id=1, source_target_pairs={{0,4},{4,8},{8,12},{12,16},{16,20},{20,24},{24,28},{28,32},{32,36}... | collective-permute-start | bytes 786440 | tf_op jit(solution)/shard_map/ppermute | solution.py:18
  30.1 4.4 %collective-permute-start.3 = (s32[256]{0:T(256)}, s32[256]{0:T(256)S(1)}, u32[]{:S(2)}, u32[]{:S(2)}) collective-permute-start(s32[256]{0:T(256)} %param.11), channel_id=1, source_target_pairs={{0,4},{4,8},{8,12},{12,16},{16,20},{20,24},{24,28},{28,32},{32,36}... | collective-permute-start | bytes 3080 | tf_op jit(solution)/shard_map/ppermute | solution.py:18
  34.4 1.9 copy.150
  36.3 4.7 %all-to-all-start.2 = ((bf16[64,4,1024]{2,0,1:T(8,128)(2,1)}), bf16[64,4,1024]{2,0,1:T(8,128)(2,1)}, u32[]{:S(2)}, u32[]{:S(2)}) async-start(bf16[64,4,1024]{2,0,1:T(8,128)(2,1)} %bitcast.108), calls=%async_computation.2 | async-start | bytes 1048576 | tf_op jit(solution)/shard_map/all_to_all | solution.py:111
  41.1 1.9 collective-permute-start.7
  43.9 2.1 collective-permute-start.2
  46.0 1.9 collective-permute-start.4
  49.6 5.1 %collective-permute-start.8 = (bf16[512,512]{1,0:T(8,128)(2,1)}, bf16[512,512]{1,0:T(8,128)(2,1)S(1)}, u32[]{:S(2)}, u32[]{:S(2)}) collective-permute-start(bf16[512,512]{1,0:T(8,128)(2,1)} %pad_maximum_fusion.3), channel_id=1, source_target_pairs={{0,8},{4,12},{8,16},{12,20},{16,24},{20,28},{24,32},{28,36},{32,40... | collective-permute-start | bytes 1572872 | tf_op jit(solution)/shard_map/ppermute | solution.py:18
  54.7 4.9 %collective-permute-done.4 = s32[256]{0:T(256)S(1)} collective-permute-done((s32[256]{0:T(256)S(1)}, s32[256]{0:T(256)S(1)}, u32[]{:S(2)}, u32[]{:S(2)}) %collective-permute-start.4) | collective-permute-done | bytes 1056 | tf_op jit(solution)/shard_map/ppermute | solution.py:18
  59.6 4.8 %collective-permute-start.5 = (s32[512]{0:T(512)S(1)}, s32[512]{0:T(512)S(1)}, u32[]{:S(2)}, u32[]{:S(2)}) collective-permute-start(s32[512]{0:T(512)S(1)} %pad_add_fusion.1), channel_id=1, source_target_pairs={{0,8},{4,12},{8,16},{12,20},{16,24},{20,28},{24,32},{28,36},{32,40... | collective-permute-start | bytes 6152 | tf_op jit(solution)/shard_map/ppermute | solution.py:18
  65.3 6.2 %collective-permute-done.5 = s32[512]{0:T(512)S(1)} collective-permute-done((s32[512]{0:T(512)S(1)}, s32[512]{0:T(512)S(1)}, u32[]{:S(2)}, u32[]{:S(2)}) %collective-permute-start.5) | collective-permute-done | bytes 2080 | tf_op jit(solution)/shard_map/ppermute | solution.py:18
  71.5 4.8 %all-to-all-start.3 = ((bf16[64,4,1024]{2,0,1:T(8,128)(2,1)}), bf16[64,4,1024]{2,0,1:T(8,128)(2,1)}, u32[]{:S(2)}, u32[]{:S(2)}) async-start(bf16[64,4,1024]{2,0,1:T(8,128)(2,1)} %bitcast.107), calls=%async_computation.3 | async-start | bytes 1048576 | tf_op jit(solution)/shard_map/all_to_all | solution.py:114
  78.7 6.9 %all-to-all-done.3 = bf16[64,4,1024]{2,0,1:T(8,128)(2,1)} async-done(((bf16[64,4,1024]{2,0,1:T(8,128)(2,1)}), bf16[64,4,1024]{2,0,1:T(8,128)(2,1)}, u32[]{:S(2)}, u32[]{:S(2)}) %all-to-all-start.3) | async-done | bytes 524320 | tf_op jit(solution)/shard_map/all_to_all | solution.py:114
  87.3 1.9 broadcast_in_dim.45.clone
  89.2 1.8 broadcast_in_dim.45
  91.0 66.6 %while.20 = (s32[]{:T(128)}, bf16[256,1024]{1,0:T(8,128)(2,1)}, bf16[256,1024]{1,0:T(8,128)(2,1)}, f32[1280,512]{1,0:T(8,128)}, f32[1280,512]{1,0:T(8,128)}, /*i...) while((s32[]{:T(128)}, bf16[256,1024]{1,0:T(8,128)(2,1)}, ...), condition=%wide.region_4.5_spmd.clone, body=%wide.region_0.4_spmd.clone.sunk | while | flops 1016857344 | bytes 32530272 | solution.py:106
  94.2 3.4 %fusion.79 = (f32[2,256]{1,0:T(2,128)S(1)}, f32[2,256,1280]{1,2,0:T(8,128)}) fusion(bf16[256,2,128]{0,2,1:T(8,128)(2,1)S(1)} %bitcast.159, pred[256,1280]{0,1:T(8,128)(4,1)S(1)} %fusion.78, bf16[1280,512]{1,0:T(8,128)(2,1)} %get-tuple-element.488, s32[]{:T(128)S(6)} %select_n.43), kind=kOutput, calls=%fused_computation.61.clone.1 | convolution fusion | flops 170394880 | bytes 3409924 | tf_op jit(solution)/shard_map/while/body/eval_jaxpr/sub | solution.py:66
  97.6 2.1 fusion.80
  101.0 1.5 fusion.81
  104.9 1.4 fusion.82
  106.3 1.4 fusion.83
  110.9 3.4 %fusion.79 = (f32[2,256]{1,0:T(2,128)S(1)}, f32[2,256,1280]{1,2,0:T(8,128)}) fusion(bf16[256,2,128]{0,2,1:T(8,128)(2,1)S(1)} %bitcast.159, pred[256,1280]{0,1:T(8,128)(4,1)S(1)} %fusion.78, bf16[1280,512]{1,0:T(8,128)(2,1)} %get-tuple-element.488, s32[]{:T(128)S(6)} %select_n.43), kind=kOutput, calls=%fused_computation.61.clone.1 | convolution fusion | flops 170394880 | bytes 3409924 | tf_op jit(solution)/shard_map/while/body/eval_jaxpr/sub | solution.py:66
  114.2 2.1 fusion.80
  117.7 1.5 fusion.81
  121.5 1.4 fusion.82
  127.5 3.4 %fusion.79 = (f32[2,256]{1,0:T(2,128)S(1)}, f32[2,256,1280]{1,2,0:T(8,128)}) fusion(bf16[256,2,128]{0,2,1:T(8,128)(2,1)S(1)} %bitcast.159, pred[256,1280]{0,1:T(8,128)(4,1)S(1)} %fusion.78, bf16[1280,512]{1,0:T(8,128)(2,1)} %get-tuple-element.488, s32[]{:T(128)S(6)} %select_n.43), kind=kOutput, calls=%fused_computation.61.clone.1 | convolution fusion | flops 170394880 | bytes 3409924 | tf_op jit(solution)/shard_map/while/body/eval_jaxpr/sub | solution.py:66
  130.8 2.1 fusion.80
  134.3 1.5 fusion.81
  138.1 1.4 fusion.82
  139.5 1.4 fusion.83
  144.1 3.4 %fusion.79 = (f32[2,256]{1,0:T(2,128)S(1)}, f32[2,256,1280]{1,2,0:T(8,128)}) fusion(bf16[256,2,128]{0,2,1:T(8,128)(2,1)S(1)} %bitcast.159, pred[256,1280]{0,1:T(8,128)(4,1)S(1)} %fusion.78, bf16[1280,512]{1,0:T(8,128)(2,1)} %get-tuple-element.488, s32[]{:T(128)S(6)} %select_n.43), kind=kOutput, calls=%fused_computation.61.clone.1 | convolution fusion | flops 170394880 | bytes 3409924 | tf_op jit(solution)/shard_map/while/body/eval_jaxpr/sub | solution.py:66
  147.5 2.1 fusion.80
  151.0 1.5 fusion.81
  154.8 1.4 fusion.82
  156.2 1.4 fusion.83
  157.6 3.5 %all-to-all-start.5 = ((bf16[4,64,1024]{2,1,0:T(8,128)(2,1)}), bf16[4,64,1024]{2,1,0:T(8,128)(2,1)S(1)}, u32[]{:S(2)}, u32[]{:S(2)}) async-start(bf16[4,64,1024]{2,1,0:T(8,128)(2,1)} %bitcast.164), calls=%async_computation.5 | async-start | bytes 1048576 | tf_op jit(solution)/shard_map/all_to_all | solution.py:160
  161.1 2.1 convert.13
  164.2 1.9 collective-permute-start.13
  166.1 1.9 collective-permute-start.16
  168.0 2.4 %collective-permute-start.15 = (bf16[256,512]{1,0:T(8,128)(2,1)}, bf16[256,512]{1,0:T(8,128)(2,1)}, u32[]{:S(2)}, u32[]{:S(2)}) collective-permute-start(bf16[256,512]{1,0:T(8,128)(2,1)} %get-tuple-element.331), channel_id=1, source_target_pairs={{12,0},{16,4},{20,8},{24,12},{28,16},{32,20},{36,24},{40,28},{44,3... | collective-permute-start | bytes 786440 | tf_op jit(solution)/shard_map/ppermute | solution.py:18
  170.4 2.7 %collective-permute-start.14 = (bf16[256,512]{1,0:T(8,128)(2,1)}, bf16[256,512]{1,0:T(8,128)(2,1)}, u32[]{:S(2)}, u32[]{:S(2)}) collective-permute-start(bf16[256,512]{1,0:T(8,128)(2,1)} %get-tuple-element.332), channel_id=1, source_target_pairs={{8,0},{12,4},{16,8},{20,12},{24,16},{28,20},{32,24},{36,28},{40,32... | collective-permute-start | bytes 786440 | tf_op jit(solution)/shard_map/ppermute | solution.py:18
  174.4 4.8 %all-to-all-start.4 = ((bf16[4,64,1024]{2,1,0:T(8,128)(2,1)}), bf16[4,64,1024]{2,1,0:T(8,128)(2,1)}, u32[]{:S(2)}, u32[]{:S(2)}) async-start(bf16[4,64,1024]{2,1,0:T(8,128)(2,1)} %bitcast.165), calls=%async_computation.4 | async-start | bytes 1048576 | tf_op jit(solution)/shard_map/all_to_all | solution.py:159
  179.1 2.2 fusion.41
  181.3 1.9 collective-permute-start.9
  183.2 4.2 %collective-permute-start.12 = (bf16[256,512]{1,0:T(8,128)(2,1)}, bf16[256,512]{1,0:T(8,128)(2,1)}, u32[]{:S(2)}, u32[]{:S(2)}) collective-permute-start(bf16[256,512]{1,0:T(8,128)(2,1)} %get-tuple-element.334), channel_id=1, source_target_pairs={{16,0},{20,4},{24,8},{28,12},{32,16},{36,20},{40,24},{44,28},{48,3... | collective-permute-start | bytes 786440 | tf_op jit(solution)/shard_map/ppermute | solution.py:18
  187.5 2.5 %collective-permute-start.11 = (bf16[256,512]{1,0:T(8,128)(2,1)}, bf16[256,512]{1,0:T(8,128)(2,1)}, u32[]{:S(2)}, u32[]{:S(2)}) collective-permute-start(bf16[256,512]{1,0:T(8,128)(2,1)} %get-tuple-element.335), channel_id=1, source_target_pairs={{12,0},{16,4},{20,8},{24,12},{28,16},{32,20},{36,24},{40,28},{44,3... | collective-permute-start | bytes 786440 | tf_op jit(solution)/shard_map/ppermute | solution.py:18
  190.0 1.9 collective-permute-start.10
  192.3 2.2 add_convert_fusion
  194.4 4.8 %all-to-all-start.7 = ((bf16[4,64,512]{2,1,0:T(8,128)(2,1)}), bf16[4,64,512]{2,1,0:T(8,128)(2,1)S(1)}, u32[]{:S(2)}, u32[]{:S(2)}) async-start(bf16[4,64,512]{2,1,0:T(8,128)(2,1)} %bitcast.14), calls=%async_computation.7 | async-start | bytes 524288 | tf_op jit(solution)/shard_map/all_to_all | solution.py:162
  199.2 3.0 %collective-permute-done.12 = bf16[256,512]{1,0:T(8,128)(2,1)} collective-permute-done((bf16[256,512]{1,0:T(8,128)(2,1)}, bf16[256,512]{1,0:T(8,128)(2,1)}, u32[]{:S(2)}, u32[]{:S(2)}) %collective-permute-start.12) | collective-permute-done | bytes 262176 | tf_op jit(solution)/shard_map/ppermute | solution.py:18
  202.2 2.7 %collective-permute-done.11 = bf16[256,512]{1,0:T(8,128)(2,1)} collective-permute-done((bf16[256,512]{1,0:T(8,128)(2,1)}, bf16[256,512]{1,0:T(8,128)(2,1)}, u32[]{:S(2)}, u32[]{:S(2)}) %collective-permute-start.11) | collective-permute-done | bytes 262176 | tf_op jit(solution)/shard_map/ppermute | solution.py:18
  204.9 7.0 %collective-permute-done.10 = bf16[256,512]{1,0:T(8,128)(2,1)} collective-permute-done((bf16[256,512]{1,0:T(8,128)(2,1)}, bf16[256,512]{1,0:T(8,128)(2,1)}, u32[]{:S(2)}, u32[]{:S(2)}) %collective-permute-start.10) | collective-permute-done | bytes 262176 | tf_op jit(solution)/shard_map/ppermute | solution.py:18
  211.9 2.1 add_convert_fusion.1
  214.0 4.8 %all-to-all-start.6 = ((bf16[4,64,512]{2,1,0:T(8,128)(2,1)}), bf16[4,64,512]{2,1,0:T(8,128)(2,1)S(1)}, u32[]{:S(2)}, u32[]{:S(2)}) async-start(bf16[4,64,512]{2,1,0:T(8,128)(2,1)} %bitcast.12), calls=%async_computation.6 | async-start | bytes 524288 | tf_op jit(solution)/shard_map/all_to_all | solution.py:161
  219.6 1.9 copy.141
  222.2 3.2 %all-to-all-done.6 = bf16[4,64,512]{2,1,0:T(8,128)(2,1)S(1)} async-done(((bf16[4,64,512]{2,1,0:T(8,128)(2,1)}), bf16[4,64,512]{2,1,0:T(8,128)(2,1)S(1)}, u32[]{:S(2)}, u32[]{:S(2)}) %all-to-all-start.6) | async-done | bytes 262176 | tf_op jit(solution)/shard_map/all_to_all | solution.py:161
  (89 shorter events, 40.9 us)
Async XLA Ops:
  2.3 11.0 %all-to-all-start = ((bf16[64,4,512]{2,0,1:T(8,128)(2,1)}), bf16[64,4,512]{2,0,1:T(8,128)(2,1)S(1)}, u32[]{:S(2)}, u32[]{:S(2)}) async-start(bf16[64,4,512]{2,0,1:T(8,128)(2,1)} %bitcast.110), calls=%async_computation | async-start | bytes 524288 | tf_op jit(solution)/shard_map/all_to_all | solution.py:113
  6.6 57.9 %copy-start.2 = (bf16[64,4096]{1,0:T(8,128)(2,1)S(1)}, bf16[64,4096]{1,0:T(8,128)(2,1)}, u32[]{:S(2)}) copy-start(bf16[64,4096]{1,0:T(8,128)(2,1)} %param.10) | copy-start | bytes 1572868
  13.3 10.1 %all-to-all-start.1 = ((bf16[64,4,512]{2,0,1:T(8,128)(2,1)}), bf16[64,4,512]{2,0,1:T(8,128)(2,1)S(1)}, u32[]{:S(2)}, u32[]{:S(2)}) async-start(bf16[64,4,512]{2,0,1:T(8,128)(2,1)} %bitcast.109), calls=%async_computation.1 | async-start | bytes 524288 | tf_op jit(solution)/shard_map/all_to_all | solution.py:112
  16.7 8.6 %collective-permute-start = (bf16[256,512]{1,0:T(8,128)(2,1)S(1)}, bf16[256,512]{1,0:T(8,128)(2,1)S(1)}, u32[]{:S(2)}, u32[]{:S(2)}) collective-permute-start(bf16[256,512]{1,0:T(8,128)(2,1)S(1)} %bitcast.166), channel_id=1, source_target_pairs={{0,4},{4,8},{8,12},{12,16},{16,20},{20,24},{24,28},{28,32},{32,36}... | collective-permute-start | bytes 786440 | tf_op jit(solution)/shard_map/ppermute | solution.py:18
  23.3 17.7 %collective-permute-start.6 = (bf16[256,512]{1,0:T(8,128)(2,1)S(1)}, bf16[256,512]{1,0:T(8,128)(2,1)S(1)}, u32[]{:S(2)}, u32[]{:S(2)}) collective-permute-start(bf16[256,512]{1,0:T(8,128)(2,1)S(1)} %bitcast.168), channel_id=1, source_target_pairs={{0,4},{4,8},{8,12},{12,16},{16,20},{20,24},{24,28},{28,32},{32,36}... | collective-permute-start | bytes 786440 | tf_op jit(solution)/shard_map/ppermute | solution.py:18
  25.3 17.8 %collective-permute-start.1 = (bf16[256,512]{1,0:T(8,128)(2,1)S(1)}, bf16[256,512]{1,0:T(8,128)(2,1)S(1)}, u32[]{:S(2)}, u32[]{:S(2)}) collective-permute-start(bf16[256,512]{1,0:T(8,128)(2,1)S(1)} %collective-permute-done), channel_id=1, source_target_pairs={{0,4},{4,8},{8,12},{12,16},{16,20},{20,24},{24,28},{28,32},{32,36}... | collective-permute-start | bytes 786440 | tf_op jit(solution)/shard_map/ppermute | solution.py:18
  30.1 16.0 %collective-permute-start.3 = (s32[256]{0:T(256)}, s32[256]{0:T(256)S(1)}, u32[]{:S(2)}, u32[]{:S(2)}) collective-permute-start(s32[256]{0:T(256)} %param.11), channel_id=1, source_target_pairs={{0,4},{4,8},{8,12},{12,16},{16,20},{20,24},{24,28},{28,32},{32,36}... | collective-permute-start | bytes 3080 | tf_op jit(solution)/shard_map/ppermute | solution.py:18
  34.4 37.0 %copy-start.3 = (s32[256]{0:T(256)S(1)}, s32[256]{0:T(256)}, u32[]{:S(2)}) copy-start(s32[256]{0:T(256)} %param.11) | copy-start | bytes 3076
  36.3 35.2 %all-to-all-start.2 = ((bf16[64,4,1024]{2,0,1:T(8,128)(2,1)}), bf16[64,4,1024]{2,0,1:T(8,128)(2,1)}, u32[]{:S(2)}, u32[]{:S(2)}) async-start(bf16[64,4,1024]{2,0,1:T(8,128)(2,1)} %bitcast.108), calls=%async_computation.2 | async-start | bytes 1048576 | tf_op jit(solution)/shard_map/all_to_all | solution.py:111
  41.1 7.7 %collective-permute-start.7 = (bf16[256,512]{1,0:T(8,128)(2,1)S(1)}, bf16[256,512]{1,0:T(8,128)(2,1)S(1)}, u32[]{:S(2)}, u32[]{:S(2)}) collective-permute-start(bf16[256,512]{1,0:T(8,128)(2,1)S(1)} %collective-permute-done.6), channel_id=1, source_target_pairs={{0,4},{4,8},{8,12},{12,16},{16,20},{20,24},{24,28},{28,32},{32,36}... | collective-permute-start | bytes 786440 | tf_op jit(solution)/shard_map/ppermute | solution.py:18
  43.9 32.4 %collective-permute-start.2 = (bf16[512,512]{1,0:T(8,128)(2,1)}, bf16[512,512]{1,0:T(8,128)(2,1)S(1)}, u32[]{:S(2)}, u32[]{:S(2)}) collective-permute-start(bf16[512,512]{1,0:T(8,128)(2,1)} %pad_maximum_fusion.2), channel_id=1, source_target_pairs={{0,8},{4,12},{8,16},{12,20},{16,24},{20,28},{24,32},{28,36},{32,40... | collective-permute-start | bytes 1572872 | tf_op jit(solution)/shard_map/ppermute | solution.py:18
  46.0 13.6 %collective-permute-start.4 = (s32[256]{0:T(256)S(1)}, s32[256]{0:T(256)S(1)}, u32[]{:S(2)}, u32[]{:S(2)}) collective-permute-start(s32[256]{0:T(256)S(1)} %collective-permute-done.3), channel_id=1, source_target_pairs={{0,4},{4,8},{8,12},{12,16},{16,20},{20,24},{24,28},{28,32},{32,36}... | collective-permute-start | bytes 3080 | tf_op jit(solution)/shard_map/ppermute | solution.py:18
  49.6 27.9 %collective-permute-start.8 = (bf16[512,512]{1,0:T(8,128)(2,1)}, bf16[512,512]{1,0:T(8,128)(2,1)S(1)}, u32[]{:S(2)}, u32[]{:S(2)}) collective-permute-start(bf16[512,512]{1,0:T(8,128)(2,1)} %pad_maximum_fusion.3), channel_id=1, source_target_pairs={{0,8},{4,12},{8,16},{12,20},{16,24},{20,28},{24,32},{28,36},{32,40... | collective-permute-start | bytes 1572872 | tf_op jit(solution)/shard_map/ppermute | solution.py:18
  59.6 11.8 %collective-permute-start.5 = (s32[512]{0:T(512)S(1)}, s32[512]{0:T(512)S(1)}, u32[]{:S(2)}, u32[]{:S(2)}) collective-permute-start(s32[512]{0:T(512)S(1)} %pad_add_fusion.1), channel_id=1, source_target_pairs={{0,8},{4,12},{8,16},{12,20},{16,24},{20,28},{24,32},{28,36},{32,40... | collective-permute-start | bytes 6152 | tf_op jit(solution)/shard_map/ppermute | solution.py:18
  71.5 14.1 %all-to-all-start.3 = ((bf16[64,4,1024]{2,0,1:T(8,128)(2,1)}), bf16[64,4,1024]{2,0,1:T(8,128)(2,1)}, u32[]{:S(2)}, u32[]{:S(2)}) async-start(bf16[64,4,1024]{2,0,1:T(8,128)(2,1)} %bitcast.107), calls=%async_computation.3 | async-start | bytes 1048576 | tf_op jit(solution)/shard_map/all_to_all | solution.py:114
  97.6 3.5 %copy-start = (f32[2,256,1280]{1,2,0:T(8,128)S(1)}, f32[2,256,1280]{1,2,0:T(8,128)}, u32[]{:S(2)}) copy-start(f32[2,256,1280]{1,2,0:T(8,128)} %get-tuple-element.434) | copy-start | bytes 7864324 | tf_op jit(solution)/shard_map/while
  114.2 3.5 %copy-start = (f32[2,256,1280]{1,2,0:T(8,128)S(1)}, f32[2,256,1280]{1,2,0:T(8,128)}, u32[]{:S(2)}) copy-start(f32[2,256,1280]{1,2,0:T(8,128)} %get-tuple-element.434) | copy-start | bytes 7864324 | tf_op jit(solution)/shard_map/while
  130.8 3.5 %copy-start = (f32[2,256,1280]{1,2,0:T(8,128)S(1)}, f32[2,256,1280]{1,2,0:T(8,128)}, u32[]{:S(2)}) copy-start(f32[2,256,1280]{1,2,0:T(8,128)} %get-tuple-element.434) | copy-start | bytes 7864324 | tf_op jit(solution)/shard_map/while
  147.5 3.5 %copy-start = (f32[2,256,1280]{1,2,0:T(8,128)S(1)}, f32[2,256,1280]{1,2,0:T(8,128)}, u32[]{:S(2)}) copy-start(f32[2,256,1280]{1,2,0:T(8,128)} %get-tuple-element.434) | copy-start | bytes 7864324 | tf_op jit(solution)/shard_map/while
  157.6 16.8 %all-to-all-start.5 = ((bf16[4,64,1024]{2,1,0:T(8,128)(2,1)}), bf16[4,64,1024]{2,1,0:T(8,128)(2,1)S(1)}, u32[]{:S(2)}, u32[]{:S(2)}) async-start(bf16[4,64,1024]{2,1,0:T(8,128)(2,1)} %bitcast.164), calls=%async_computation.5 | async-start | bytes 1048576 | tf_op jit(solution)/shard_map/all_to_all | solution.py:160
  161.1 12.0 %copy-start.1 = (f32[1280,512]{1,0:T(8,128)S(1)}, f32[1280,512]{1,0:T(8,128)}, u32[]{:S(2)}) copy-start(f32[1280,512]{1,0:T(8,128)} %get-tuple-element.178) | copy-start | bytes 7864324
  164.2 19.1 %collective-permute-start.13 = (bf16[256,512]{1,0:T(8,128)(2,1)}, bf16[256,512]{1,0:T(8,128)(2,1)S(1)}, u32[]{:S(2)}, u32[]{:S(2)}) collective-permute-start(bf16[256,512]{1,0:T(8,128)(2,1)} %get-tuple-element.329), channel_id=1, source_target_pairs={{4,0},{8,4},{12,8},{16,12},{20,16},{24,20},{28,24},{32,28},{36,32}... | collective-permute-start | bytes 786440 | tf_op jit(solution)/shard_map/ppermute | solution.py:18
  166.1 21.4 %collective-permute-start.16 = (bf16[256,512]{1,0:T(8,128)(2,1)}, bf16[256,512]{1,0:T(8,128)(2,1)}, u32[]{:S(2)}, u32[]{:S(2)}) collective-permute-start(bf16[256,512]{1,0:T(8,128)(2,1)} %get-tuple-element.330), channel_id=1, source_target_pairs={{16,0},{20,4},{24,8},{28,12},{32,16},{36,20},{40,24},{44,28},{48,3... | collective-permute-start | bytes 786440 | tf_op jit(solution)/shard_map/ppermute | solution.py:18
  168.0 22.0 %collective-permute-start.15 = (bf16[256,512]{1,0:T(8,128)(2,1)}, bf16[256,512]{1,0:T(8,128)(2,1)}, u32[]{:S(2)}, u32[]{:S(2)}) collective-permute-start(bf16[256,512]{1,0:T(8,128)(2,1)} %get-tuple-element.331), channel_id=1, source_target_pairs={{12,0},{16,4},{20,8},{24,12},{28,16},{32,20},{36,24},{40,28},{44,3... | collective-permute-start | bytes 786440 | tf_op jit(solution)/shard_map/ppermute | solution.py:18
  170.4 21.9 %collective-permute-start.14 = (bf16[256,512]{1,0:T(8,128)(2,1)}, bf16[256,512]{1,0:T(8,128)(2,1)}, u32[]{:S(2)}, u32[]{:S(2)}) collective-permute-start(bf16[256,512]{1,0:T(8,128)(2,1)} %get-tuple-element.332), channel_id=1, source_target_pairs={{8,0},{12,4},{16,8},{20,12},{24,16},{28,20},{32,24},{36,28},{40,32... | collective-permute-start | bytes 786440 | tf_op jit(solution)/shard_map/ppermute | solution.py:18
  174.4 20.0 %all-to-all-start.4 = ((bf16[4,64,1024]{2,1,0:T(8,128)(2,1)}), bf16[4,64,1024]{2,1,0:T(8,128)(2,1)}, u32[]{:S(2)}, u32[]{:S(2)}) async-start(bf16[4,64,1024]{2,1,0:T(8,128)(2,1)} %bitcast.165), calls=%async_computation.4 | async-start | bytes 1048576 | tf_op jit(solution)/shard_map/all_to_all | solution.py:159
  181.3 17.9 %collective-permute-start.9 = (bf16[256,512]{1,0:T(8,128)(2,1)}, bf16[256,512]{1,0:T(8,128)(2,1)}, u32[]{:S(2)}, u32[]{:S(2)}) collective-permute-start(bf16[256,512]{1,0:T(8,128)(2,1)} %get-tuple-element.333), channel_id=1, source_target_pairs={{4,0},{8,4},{12,8},{16,12},{20,16},{24,20},{28,24},{32,28},{36,32}... | collective-permute-start | bytes 786440 | tf_op jit(solution)/shard_map/ppermute | solution.py:18
  183.2 19.0 %collective-permute-start.12 = (bf16[256,512]{1,0:T(8,128)(2,1)}, bf16[256,512]{1,0:T(8,128)(2,1)}, u32[]{:S(2)}, u32[]{:S(2)}) collective-permute-start(bf16[256,512]{1,0:T(8,128)(2,1)} %get-tuple-element.334), channel_id=1, source_target_pairs={{16,0},{20,4},{24,8},{28,12},{32,16},{36,20},{40,24},{44,28},{48,3... | collective-permute-start | bytes 786440 | tf_op jit(solution)/shard_map/ppermute | solution.py:18
  187.5 17.4 %collective-permute-start.11 = (bf16[256,512]{1,0:T(8,128)(2,1)}, bf16[256,512]{1,0:T(8,128)(2,1)}, u32[]{:S(2)}, u32[]{:S(2)}) collective-permute-start(bf16[256,512]{1,0:T(8,128)(2,1)} %get-tuple-element.335), channel_id=1, source_target_pairs={{12,0},{16,4},{20,8},{24,12},{28,16},{32,20},{36,24},{40,28},{44,3... | collective-permute-start | bytes 786440 | tf_op jit(solution)/shard_map/ppermute | solution.py:18
  190.0 21.9 %collective-permute-start.10 = (bf16[256,512]{1,0:T(8,128)(2,1)}, bf16[256,512]{1,0:T(8,128)(2,1)}, u32[]{:S(2)}, u32[]{:S(2)}) collective-permute-start(bf16[256,512]{1,0:T(8,128)(2,1)} %get-tuple-element.336), channel_id=1, source_target_pairs={{8,0},{12,4},{16,8},{20,12},{24,16},{28,20},{32,24},{36,28},{40,32... | collective-permute-start | bytes 786440 | tf_op jit(solution)/shard_map/ppermute | solution.py:18
  194.4 19.6 %all-to-all-start.7 = ((bf16[4,64,512]{2,1,0:T(8,128)(2,1)}), bf16[4,64,512]{2,1,0:T(8,128)(2,1)S(1)}, u32[]{:S(2)}, u32[]{:S(2)}) async-start(bf16[4,64,512]{2,1,0:T(8,128)(2,1)} %bitcast.14), calls=%async_computation.7 | async-start | bytes 524288 | tf_op jit(solution)/shard_map/all_to_all | solution.py:162
  214.0 11.5 %all-to-all-start.6 = ((bf16[4,64,512]{2,1,0:T(8,128)(2,1)}), bf16[4,64,512]{2,1,0:T(8,128)(2,1)S(1)}, u32[]{:S(2)}, u32[]{:S(2)}) async-start(bf16[4,64,512]{2,1,0:T(8,128)(2,1)} %bitcast.12), calls=%async_computation.6 | async-start | bytes 524288 | tf_op jit(solution)/shard_map/all_to_all | solution.py:161
where the time goes:
time: 228 us; the launch traced here: 226 us
  starting transfers between devices  83.4 us (37%)
  waiting for transfers between devices  44.7 us (20%)
  matrix products  41.5 us (18%)
  local copies, waits for them, and re-layouts  30.7 us (13%)
  other arithmetic  24.5 us (11%)
    ppermute x17, starting transfers between devices, from_behind(): return lax.ppermute(block, axis, route)  48.4 us
    ppermute x17, waiting for transfers between devices, from_behind(): return lax.ppermute(block, axis, route)  24.9 us
    sub x4, matrix products, one_group(): weights = jnp.exp(masked - highest)  13.5 us
    convert_element_type x4, other arithmetic, one_group(): probs_low = probs.astype(jnp.bfloat16)  8.42 us
    all_to_all x1, waiting for transfers between devices, body(): lax.all_to_all(grad_out, 'head', split_axis=1, concat_axis=0, tiled=True)  6.9 us
    dot_general x4, matrix products, one_group(): jnp.einsum('and,cd->nac', block_grads, block_values, preferred_element_ty...  6.11 us
    dot_general x4, matrix products, one_group(): jnp.einsum('nac,and->cd', score_grads, block_queries, preferred_element_t...  5.57 us
    dot_general x4, matrix products, one_group(): jnp.einsum('nac,and->cd', probs_low, block_grads, preferred_element_type=...  5.55 us
  transfers between devices with their start and end apart: 25, of which 11 were waited for; matrix products, arithmetic and copies ran while one was open for 10% of the time, Pallas kernels for 0%

commit v1 on v0

v1 whole, which is shorter than its diff:
```python
import functools
import math

import jax
import jax.numpy as jnp
from jax import lax
from jax.experimental import pallas as pl
from jax.experimental.pallas import tpu as pltpu
from jax.sharding import PartitionSpec as P

QHEADS = 32
KVHEADS = 16
HEAD_DIM = 128
WINDOW = 1024
DOCS = 8

ATTN_SCALE = 168.0 ** (-0.5)
EXP2_SCALE = ATTN_SCALE * math.log2(math.e)
MESH = pl.DeviceIdType.MESH

ROWS = 64
TILE = 256
STEPS = WINDOW // TILE
SPAN = WINDOW + TILE
PAIR = 2 * HEAD_DIM
HIDDEN = -1e30


def dot(a, b, dims=((1,), (0,))):
    return lax.dot_general(a, b, (dims, ((), ())), preferred_element_type=jnp.float32)


def await_bytes(ref, sem):
    pltpu.make_async_copy(ref, ref, sem).wait()


def kernel(
    q_ref, k_ref, v_ref, g_ref, seg_ref,
    a_ref, gq_ref, gk_ref, gv_ref,
    qb, kb, vb, gb, segb,
    kt, vt, pb, ot, lo_buf, ab, gqb, dk_acc, dv_acc, dk_out, dv_out, dk_in, dv_in, gkb, gvb,
    send, recv, ring_send, ring_recv, out_send, out_recv,
):
    ctx, x = lax.axis_index("ctx"), lax.axis_index("head")
    core, y, z = ctx % 2, (ctx // 2) % 4, ctx // 8
    planes = lax.axis_size("ctx") // 8
    half = y // 2
    slot = ((y % 2) * 2 + core) * 4 + x
    group = x * 4 + y
    after = (jnp.where(core == 0, ctx + 1, ((z + 1) % planes) * 8 + y * 2), x)
    before = (jnp.where(core == 1, ctx - 1, ((z + planes - 1) % planes) * 8 + y * 2 + 1), x)
    stays = half == core

    def source(yy, c, dx):
        return ((z * 4 + core * 2 + yy) * 2 + c, (x + dx) % 4)

    barrier = pltpu.get_barrier_semaphore()
    for yy in range(2):
        for c in range(2):
            for dx in range(4):
                pl.semaphore_signal(barrier, inc=1, device_id=source(yy, c, dx), device_id_type=MESH)
    pl.semaphore_signal(barrier, inc=1, device_id=before, device_id_type=MESH)
    pl.semaphore_wait(barrier, 17)

    def target(dx, dy):
        tx, ty = (x + dx) % 4, (y + dy) % 4
        return ((z * 4 + ty) * 2 + half, tx), tx * 4 + ty

    def ship(src, dst, send_sem, recv_sem, where, local):
        def far():
            pltpu.make_async_remote_copy(
                src_ref=src, dst_ref=dst, send_sem=send_sem, recv_sem=recv_sem,
                device_id=where, device_id_type=MESH,
            ).start()

        if local is None:
            far()
        else:
            pl.when(local)(lambda: pltpu.make_async_copy(src, dst, recv_sem).start())
            pl.when(jnp.logical_not(local))(far)

    offsets = [(dx, dy) for dx in (2, 1, 3, 0) for dy in (2, 1, 3, 0)]
    own_rows = pl.ds(pl.multiple_of(slot * ROWS, ROWS), ROWS)
    own_rows2 = pl.ds(pl.multiple_of(WINDOW + slot * ROWS, ROWS), ROWS)
    for dy in range(4):
        where, _ = target(0, dy)
        ship(
            seg_ref, segb.at[STEPS + (y % 2) * 2 + core], send.at[4], recv.at[4],
            where, stays if dy == 0 else None,
        )
    for index, (src, dst, width, rows) in enumerate(
        (
            (k_ref, kb, HEAD_DIM, own_rows2),
            (v_ref, vb, HEAD_DIM, own_rows2),
            (q_ref, qb, PAIR, own_rows),
            (g_ref, gb, PAIR, own_rows),
        )
    ):
        for dx, dy in offsets:
            where, head = target(dx, dy)
            ship(
                src.at[:, pl.ds(pl.multiple_of(head * width, width), width)],
                dst.at[rows, :],
                send.at[index],
                recv.at[index],
                where,
                stays if dx == 0 and dy == 0 else None,
            )

    newer, older = pl.ds(WINDOW, WINDOW), pl.ds(0, WINDOW)
    ring = []
    for index, (buf, here, there) in enumerate(
        (
            (segb, pl.ds(STEPS, STEPS), pl.ds(0, STEPS)),
            (kb, newer, older),
            (vb, newer, older),
        )
    ):
        await_bytes(buf.at[here], recv.at[(4, 0, 1)[index]])
        copy = pltpu.make_async_remote_copy(
            src_ref=buf.at[here], dst_ref=buf.at[there],
            send_sem=ring_send.at[index], recv_sem=ring_recv.at[index],
            device_id=after, device_id_type=MESH,
        )
        copy.start()
        ring.append(copy)

    ring[0].wait()
    rows = [segb[r].astype(jnp.float32) for r in range(2 * STEPS)]
    for r in range(STEPS):
        rows[r] = jnp.where(ctx < 0, rows[r], jnp.where((z == 0) & (core == 0), -1.0, rows[r]))
    all_rows = jnp.concatenate(rows, axis=0)
    starts = [
        jnp.sum(
            jnp.sum((all_rows < d).astype(jnp.float32), axis=0, keepdims=True), axis=1, keepdims=True
        )
        for d in range(DOCS)
    ]
    lane = lax.broadcasted_iota(jnp.int32, (1, TILE), 1).astype(jnp.float32)
    for i in range(STEPS):
        row = rows[STEPS + i]
        first = jnp.maximum(lane + (i * TILE + 1.0), 0.0)
        for d in range(DOCS):
            first = jnp.maximum(first, jnp.where(row >= d, starts[d], 0.0))
        lo_buf[i] = (first - i * TILE).astype(jnp.int32)

    dk_acc[...] = jnp.zeros_like(dk_acc)
    dv_acc[...] = jnp.zeros_like(dv_acc)
    ring[1].wait()
    kt[...] = kb[...].T
    ring[2].wait()
    vt[...] = vb[...].T
    await_bytes(qb, recv.at[2])

    key_index = lax.broadcasted_iota(jnp.int32, (SPAN, TILE), 0)
    last_key = WINDOW + lax.broadcasted_iota(jnp.int32, (1, TILE), 1)

    def forward(i, carry):
        base = pl.multiple_of(i * TILE, TILE)
        keys = kb[pl.ds(base, SPAN), :]
        values_t = vt[:, pl.ds(base, SPAN)]
        seen = (key_index >= lo_buf[i]) & (key_index <= last_key)
        for n in range(2):
            columns = slice(n * HEAD_DIM, (n + 1) * HEAD_DIM)
            scores = dot(keys, qb[pl.ds(base, TILE), columns], ((1,), (1,)))
            scores = jnp.where(seen, scores, HIDDEN)
            top = jnp.max(scores, axis=0, keepdims=True)
            weights = jnp.exp2(scores * EXP2_SCALE - top * EXP2_SCALE)
            total = jnp.sum(weights, axis=0, keepdims=True)
            probs = (weights * (1.0 / total)).astype(jnp.bfloat16)
            pb[i, :, n * TILE : (n + 1) * TILE] = probs
            out_t = dot(values_t, probs)
            ot[n, i] = out_t
            ab[pl.ds(base, TILE), columns] = out_t.T.astype(jnp.bfloat16)
        for dx in range(4):
            send_back(ab, a_ref, PAIR, i, dx, 0)
        return carry

    def send_back(buf, out, width, i, dx, index):
        yy, c = i // 2, i % 2
        tx = (x + dx) % 4
        ty = core * 2 + yy
        where = ((z * 4 + ty) * 2 + c, tx)
        ship(
            buf.at[pl.ds(pl.multiple_of((i * 4 + tx) * ROWS, ROWS), ROWS), :],
            out.at[:, pl.ds(pl.multiple_of(group * width, width), width)],
            out_send.at[index],
            out_recv.at[index],
            where,
            ((ty == y) & (c == core)) if dx == 0 else None,
        )

    lax.fori_loop(0, STEPS, forward, 0)
    await_bytes(gb, recv.at[3])

    def backward(i, carry):
        base = pl.multiple_of(i * TILE, TILE)
        span = pl.ds(base, SPAN)
        values = vb[span, :]
        parts = []
        for n in range(2):
            columns = slice(n * HEAD_DIM, (n + 1) * HEAD_DIM)
            probs = pb[i, :, n * TILE : (n + 1) * TILE]
            grads_t = gb[pl.ds(base, TILE), columns].T
            low = ot[n, i].astype(jnp.bfloat16).astype(jnp.float32)
            delta = jnp.sum(low * grads_t.astype(jnp.float32), axis=0, keepdims=True)
            prob_grads = dot(values, grads_t)
            score_grads = (probs.astype(jnp.float32) * (prob_grads - delta)).astype(jnp.bfloat16)
            dq_t = dot(kt[:, span], score_grads) * ATTN_SCALE
            gqb[pl.ds(base, TILE), columns] = dq_t.T.astype(jnp.bfloat16)
            dv_acc[span, :] += dot(probs, gb[pl.ds(base, TILE), columns])
            dk_acc[span, :] += dot(score_grads, qb[pl.ds(base, TILE), columns])
        for dx in range(4):
            send_back(gqb, gq_ref, PAIR, i, dx, 1)
        return carry

    lax.fori_loop(0, STEPS, backward, 0)

    dk_out[...] = (dk_acc[older, :] * ATTN_SCALE).astype(jnp.bfloat16)
    dv_out[...] = dv_acc[older, :].astype(jnp.bfloat16)
    back = []
    for index, (src, dst) in enumerate(((dk_out, dk_in), (dv_out, dv_in))):
        copy = pltpu.make_async_remote_copy(
            src_ref=src, dst_ref=dst, send_sem=ring_send.at[3 + index], recv_sem=ring_recv.at[3 + index],
            device_id=before, device_id_type=MESH,
        )
        copy.start()
        back.append(copy)
    back[0].wait()
    gkb[...] = (dk_acc[newer, :] * ATTN_SCALE + dk_in[...].astype(jnp.float32)).astype(jnp.bfloat16)
    for i in range(STEPS):
        for dx in range(4):
            send_back(gkb, gk_ref, HEAD_DIM, i, dx, 2)
    back[1].wait()
    gvb[...] = (dv_acc[newer, :] + dv_in[...].astype(jnp.float32)).astype(jnp.bfloat16)
    for i in range(STEPS):
        for dx in range(4):
            send_back(gvb, gv_ref, HEAD_DIM, i, dx, 3)

    for index, out in enumerate((a_ref, gq_ref, gk_ref, gv_ref)):
        await_bytes(out, out_recv.at[index])
    for index, ref in enumerate((k_ref, v_ref, q_ref, g_ref)):
        width = ref.shape[1] // 16
        await_bytes(ref.at[:, pl.ds(0, 15 * width)], send.at[index])
        pl.when(jnp.logical_not(stays))(
            functools.partial(await_bytes, ref.at[:, pl.ds(0, width)], send.at[index])
        )
    for _ in range(3):
        await_bytes(seg_ref, send.at[4])
    pl.when(jnp.logical_not(stays))(functools.partial(await_bytes, seg_ref, send.at[4]))
    for index, buf in enumerate((ab, gqb, gkb, gvb)):
        await_bytes(buf.at[pl.ds(0, 15 * ROWS), :], out_send.at[index])
        pl.when(jnp.logical_not(stays))(
            functools.partial(await_bytes, buf.at[pl.ds(0, ROWS), :], out_send.at[index])
        )


def body(queries, keys, values, grad_out, segments):
    low = jnp.bfloat16
    shape = jax.ShapeDtypeStruct
    return pl.pallas_call(
        kernel,
        out_shape=(
            shape(queries.shape, low),
            shape(queries.shape, low),
            shape(keys.shape, low),
            shape(keys.shape, low),
        ),
        in_specs=[pl.BlockSpec(memory_space=pltpu.VMEM)] * 5,
        out_specs=[pl.BlockSpec(memory_space=pltpu.VMEM)] * 4,
        scratch_shapes=[
            pltpu.VMEM((WINDOW, PAIR), low),
            pltpu.VMEM((2 * WINDOW, HEAD_DIM), low),
            pltpu.VMEM((2 * WINDOW, HEAD_DIM), low),
            pltpu.VMEM((WINDOW, PAIR), low),
            pltpu.VMEM((2 * STEPS, 1, TILE), jnp.int32),
            pltpu.VMEM((HEAD_DIM, 2 * WINDOW), low),
            pltpu.VMEM((HEAD_DIM, 2 * WINDOW), low),
            pltpu.VMEM((STEPS, SPAN, 2 * TILE), low),
            pltpu.VMEM((2, STEPS, HEAD_DIM, TILE), jnp.float32),
            pltpu.VMEM((STEPS, 1, TILE), jnp.int32),
            pltpu.VMEM((WINDOW, PAIR), low),
            pltpu.VMEM((WINDOW, PAIR), low),
            pltpu.VMEM((2 * WINDOW, HEAD_DIM), jnp.float32),
            pltpu.VMEM((2 * WINDOW, HEAD_DIM), jnp.float32),
            pltpu.VMEM((WINDOW, HEAD_DIM), low),
            pltpu.VMEM((WINDOW, HEAD_DIM), low),
            pltpu.VMEM((WINDOW, HEAD_DIM), low),
            pltpu.VMEM((WINDOW, HEAD_DIM), low),
            pltpu.VMEM((WINDOW, HEAD_DIM), low),
            pltpu.VMEM((WINDOW, HEAD_DIM), low),
            pltpu.SemaphoreType.DMA((5,)),
            pltpu.SemaphoreType.DMA((5,)),
            pltpu.SemaphoreType.DMA((5,)),
            pltpu.SemaphoreType.DMA((5,)),
            pltpu.SemaphoreType.DMA((4,)),
            pltpu.SemaphoreType.DMA((4,)),
        ],
        compiler_params=pltpu.CompilerParams(
            collective_id=0, has_side_effects=True, vmem_limit_bytes=56 * 1024 * 1024
        ),
    )(queries, keys, values, grad_out, segments.reshape(1, TILE))


def solution(mesh):
    spec = P(("ctx", "head"), None)
    return jax.shard_map(
        body,
        mesh=mesh,
        in_specs=(spec, spec, spec, spec, P("ctx")),
        out_specs=(spec, spec, spec, spec),
        check_vma=False,
    )
```

time: 228 us -> 63.8 us (0.28)
  the two profiles are of different devices: /device:TPU:120 before, /device:TPU:1 now
where the time goes in v1:
time: 63.8 us; the launch traced here: 63.6 us
  Pallas kernels  58.2 us (91%)
  local copies, waits for them, and re-layouts  4.77 us (7%)
  between operations  0.65 us (1%)
    pallas_call x1, Pallas kernels, body(): pl.pallas_call(kernel, out_shape=(shape(queries.shape, low), shape(querie...  58.2 us
    unnamed x10, local copies, waits for them, and re-layouts  4.77 us

profile of v1, /device:TPU:1, one launch (start us, length us, event | category | flops | bytes accessed | tf_op | source)
XLA Modules:
  0.0 63.6 jit_solution(12072429867914644019)
XLA Ops:
  0.6 58.2 %shard_map.84 = (bf16[64,4096]{1,0:T(8,128)(2,1)}, bf16[64,4096]{1,0:T(8,128)(2,1)}, bf16[64,2048]{1,0:T(8,128)(2,1)}, bf16[64,2048]{1,0:T(8,128)(2,1)}) custom-call(bf16[64,4096]{1,0:T(8,128)(2,1)} %q_ref.1, bf16[64,2048]{1,0:T(8,128)(2,1)} %k_ref.1, bf16[64,2048]{1,0:T(8,128)(2,1)} %v_ref.1, bf16[64,4096]{1,0:T(8,128)(2,1)} %g_ref.1, s32[1,256]{1,0:T(1,128)} %bitcast.1), custom_call_target="tpu_custom_call" | custom-call | tf_op jit(solution)/shard_map/pallas_call | solution.py:261
  58.8 0.0 copy-start
  58.8 1.9 %copy.13 = bf16[64,4096]{1,0:T(8,128)(2,1)} copy(bf16[64,4096]{1,0:T(8,128)(2,1)} %get-tuple-element.8) | data formatting | bytes 1048576
  60.7 0.0 copy-done
  60.8 0.0 copy-start.2
  60.8 0.8 %copy.14 = bf16[64,4096]{1,0:T(8,128)(2,1)} copy(bf16[64,4096]{1,0:T(8,128)(2,1)S(1)} %copy-done) | data formatting | bytes 1048576
  61.5 0.3 copy-done.2
  61.8 0.0 copy-start.1
  61.8 0.7 %copy.15 = bf16[64,2048]{1,0:T(8,128)(2,1)} copy(bf16[64,2048]{1,0:T(8,128)(2,1)S(1)} %copy-done.2) | data formatting | bytes 524288
  62.5 0.3 copy-done.1
  62.9 0.7 %copy.16 = bf16[64,2048]{1,0:T(8,128)(2,1)} copy(bf16[64,2048]{1,0:T(8,128)(2,1)S(1)} %copy-done.1) | data formatting | bytes 524288
Async XLA Ops:
  58.8 1.9 %copy-start = (bf16[64,4096]{1,0:T(8,128)(2,1)S(1)}, bf16[64,4096]{1,0:T(8,128)(2,1)}, u32[]{:S(2)}) copy-start(bf16[64,4096]{1,0:T(8,128)(2,1)} %get-tuple-element.9) | copy-start | bytes 1572868
  60.8 1.1 %copy-start.2 = (bf16[64,2048]{1,0:T(8,128)(2,1)S(1)}, bf16[64,2048]{1,0:T(8,128)(2,1)}, u32[]{:S(2)}) copy-start(bf16[64,2048]{1,0:T(8,128)(2,1)} %get-tuple-element.10) | copy-start | bytes 786436
  61.8 1.0 %copy-start.1 = (bf16[64,2048]{1,0:T(8,128)(2,1)S(1)}, bf16[64,2048]{1,0:T(8,128)(2,1)}, u32[]{:S(2)}) copy-start(bf16[64,2048]{1,0:T(8,128)(2,1)} %get-tuple-element.11) | copy-start | bytes 786436

commit v2 on v1

v2 whole, which is shorter than its diff:
```python
import functools
import math

import jax
import jax.numpy as jnp
from jax import lax
from jax.experimental import pallas as pl
from jax.experimental.pallas import tpu as pltpu
from jax.sharding import PartitionSpec as P

QHEADS = 32
KVHEADS = 16
HEAD_DIM = 128
WINDOW = 1024
DOCS = 8

ATTN_SCALE = 168.0 ** (-0.5)
EXP2_SCALE = ATTN_SCALE * math.log2(math.e)
MESH = pl.DeviceIdType.MESH

ROWS = 64
TILE = 256
STEPS = WINDOW // TILE
SPAN = WINDOW + TILE
HIDDEN = -1e30


def dot(a, b, dims=((1,), (0,))):
    return lax.dot_general(a, b, (dims, ((), ())), preferred_element_type=jnp.float32)


def await_bytes(ref, sem):
    pltpu.make_async_copy(ref, ref, sem).wait()


def kernel(
    q_ref, k_ref, v_ref, g_ref, seg_ref,
    a_ref, gq_ref, gk_ref, gv_ref,
    q_own, k_own, v_own, g_own,
    qb, kb, vb, gb, segb,
    kt, vt, pb, ot, dq, lo_buf, ab, gqb, dk_acc, dv_acc, dk_out, dv_out, dk_in, dv_in, gkb, gvb,
    load, send, recv, ring_send, ring_recv, out_send, out_recv,
):
    ctx, x = lax.axis_index("ctx"), lax.axis_index("head")
    core, y, z = ctx % 2, (ctx // 2) % 4, ctx // 8
    planes = lax.axis_size("ctx") // 8
    half = y // 2
    slot = ((y % 2) * 2 + core) * 4 + x
    group = x * 4 + y
    has_after = (z < planes - 1) | (core == 0)
    has_before = (z > 0) | (core == 1)
    after = (jnp.where(core == 0, ctx + 1, ((z + 1) % planes) * 8 + y * 2), x)
    before = (jnp.where(core == 1, ctx - 1, ((z + planes - 1) % planes) * 8 + y * 2 + 1), x)
    stays = half == core
    leaves = jnp.logical_not(stays)

    def source(yy, c, dx):
        return ((z * 4 + core * 2 + yy) * 2 + c, (x + dx) % 4)

    barrier = pltpu.get_barrier_semaphore()
    for yy in range(2):
        for c in range(2):
            for dx in range(4):
                pl.semaphore_signal(barrier, inc=1, device_id=source(yy, c, dx), device_id_type=MESH)

    @pl.when(has_before)
    def _():
        pl.semaphore_signal(barrier, inc=1, device_id=before, device_id_type=MESH)

    loads = [
        pltpu.make_async_copy(src, dst, load.at[n])
        for n, (src, dst) in enumerate(
            ((k_ref, k_own), (v_ref, v_own), (q_ref, q_own), (g_ref, g_own))
        )
    ]
    for copy in loads:
        copy.start()
    newer, older = pl.ds(WINDOW, WINDOW), pl.ds(0, WINDOW)

    @pl.when(jnp.logical_not(has_before))
    def _():
        kb[older, :] = jnp.zeros((WINDOW, HEAD_DIM), kb.dtype)
        vb[older, :] = jnp.zeros((WINDOW, HEAD_DIM), vb.dtype)
        segb[pl.ds(0, STEPS)] = jnp.full((STEPS, 1, TILE), -1, segb.dtype)

    pl.semaphore_wait(barrier, 16 + has_after.astype(jnp.int32))

    def target(dx, dy):
        tx, ty = (x + dx) % 4, (y + dy) % 4
        return ((z * 4 + ty) * 2 + half, tx), tx * 4 + ty

    def ship(src, dst, send_sem, recv_sem, where, local):
        def far():
            pltpu.make_async_remote_copy(
                src_ref=src, dst_ref=dst, send_sem=send_sem, recv_sem=recv_sem,
                device_id=where, device_id_type=MESH,
            ).start()

        if local is None:
            far()
        else:
            pl.when(local)(lambda: pltpu.make_async_copy(src, dst, recv_sem).start())
            pl.when(jnp.logical_not(local))(far)

    offsets = [(dx, dy) for dx in range(4) for dy in range(4)]
    offsets = sorted(offsets, key=lambda o: min(o[0], 4 - o[0]) + min(o[1], 4 - o[1]))
    own_rows = pl.ds(pl.multiple_of(slot * ROWS, ROWS), ROWS)
    own_rows2 = pl.ds(pl.multiple_of(WINDOW + slot * ROWS, ROWS), ROWS)
    for dy in range(4):
        where, _ = target(0, dy)
        ship(
            seg_ref, segb.at[STEPS + (y % 2) * 2 + core], send.at[6], recv.at[6],
            where, stays if dy == 0 else None,
        )
    streams = (
        (k_own, kb, own_rows2, 1, 0, 0),
        (v_own, vb, own_rows2, 1, 0, 1),
        (q_own, qb.at[0], own_rows, 2, 0, 2),
        (q_own, qb.at[1], own_rows, 2, 1, None),
        (g_own, gb.at[0], own_rows, 2, 0, 3),
        (g_own, gb.at[1], own_rows, 2, 1, None),
    )
    for index, (src, dst, rows, per, n, loaded) in enumerate(streams):
        if loaded is not None:
            loads[loaded].wait()
        for dx, dy in offsets:
            where, head = target(dx, dy)
            column = (head * per + n) * HEAD_DIM
            ship(
                src.at[:, pl.ds(pl.multiple_of(column, HEAD_DIM), HEAD_DIM)],
                dst.at[rows, :],
                send.at[index],
                recv.at[index],
                where,
                stays if dx == 0 and dy == 0 else None,
            )

    ring = []
    for index, (buf, here, there) in enumerate(
        (
            (segb, pl.ds(STEPS, STEPS), pl.ds(0, STEPS)),
            (kb, newer, older),
            (vb, newer, older),
        )
    ):
        await_bytes(buf.at[here], recv.at[(6, 0, 1)[index]])
        copy = pltpu.make_async_remote_copy(
            src_ref=buf.at[here], dst_ref=buf.at[there],
            send_sem=ring_send.at[index], recv_sem=ring_recv.at[index],
            device_id=after, device_id_type=MESH,
        )
        pl.when(has_after)(copy.start)
        ring.append(copy)

    kt[:, newer] = kb[newer, :].T
    vt[:, newer] = vb[newer, :].T
    dk_acc[...] = jnp.zeros_like(dk_acc)
    dv_acc[...] = jnp.zeros_like(dv_acc)
    pl.when(has_before)(ring[0].wait_recv)
    rows = [segb[r].astype(jnp.float32) for r in range(2 * STEPS)]
    all_rows = jnp.concatenate(rows, axis=0)
    starts = [
        jnp.sum(
            jnp.sum((all_rows < d).astype(jnp.float32), axis=0, keepdims=True), axis=1, keepdims=True
        )
        for d in range(DOCS)
    ]
    lane = lax.broadcasted_iota(jnp.int32, (1, TILE), 1).astype(jnp.float32)
    for i in range(STEPS):
        row = rows[STEPS + i]
        first = lane + (i * TILE + 1.0)
        for d in range(DOCS):
            first = jnp.maximum(first, jnp.where(row >= d, starts[d], 0.0))
        lo_buf[i] = (first - i * TILE).astype(jnp.int32)
    pl.when(has_before)(ring[1].wait_recv)
    kt[:, older] = kb[older, :].T
    pl.when(has_before)(ring[2].wait_recv)
    vt[:, older] = vb[older, :].T

    key_index = lax.broadcasted_iota(jnp.int32, (SPAN, TILE), 0)
    last_key = WINDOW + lax.broadcasted_iota(jnp.int32, (1, TILE), 1)

    def send_back(buf, out, per, n, i, dx, index):
        yy, c = i // 2, i % 2
        tx = (x + dx) % 4
        ty = core * 2 + yy
        where = ((z * 4 + ty) * 2 + c, tx)
        ship(
            buf.at[pl.ds(pl.multiple_of((i * 4 + tx) * ROWS, ROWS), ROWS), :],
            out.at[:, pl.ds(pl.multiple_of((group * per + n) * HEAD_DIM, HEAD_DIM), HEAD_DIM)],
            out_send.at[index],
            out_recv.at[index],
            where,
            ((ty == y) & (c == core)) if dx == 0 else None,
        )

    def forward(n):
        def step(j, carry):
            for i in (2 * j, 2 * j + 1):
                base = pl.multiple_of(i * TILE, TILE)
                seen = (key_index >= lo_buf[i]) & (key_index <= last_key)
                scores = dot(kb[pl.ds(base, SPAN), :], qb[n, pl.ds(base, TILE), :], ((1,), (1,)))
                scores = jnp.where(seen, scores, HIDDEN)
                top = jnp.max(scores, axis=0, keepdims=True)
                weights = jnp.exp2(scores * EXP2_SCALE - top * EXP2_SCALE)
                total = jnp.sum(weights, axis=0, keepdims=True)
                probs = (weights * (1.0 / total)).astype(jnp.bfloat16)
                pb[n, i] = probs
                out_t = dot(vt[:, pl.ds(base, SPAN)], probs)
                ot[n, i] = out_t
                ab[n, pl.ds(base, TILE), :] = out_t.T.astype(jnp.bfloat16)
            for i in (2 * j, 2 * j + 1):
                for dx in range(4):
                    send_back(ab.at[n], a_ref, 2, n, i, dx, n)
            return carry

        lax.fori_loop(0, STEPS // 2, step, 0)

    def grads_of(n, i):
        base = pl.multiple_of(i * TILE, TILE)
        grads = gb[n, pl.ds(base, TILE), :]
        grads_t = grads.T
        low = ot[n, i].astype(jnp.bfloat16).astype(jnp.float32)
        delta = jnp.sum(low * grads_t.astype(jnp.float32), axis=0, keepdims=True)
        return base, grads, grads_t, delta

    def part(n, i, base, first, count, grads, grads_t, delta):
        span = pl.ds(pl.multiple_of(base + first, TILE), count)
        probs = pb[n, i, first : first + count, :]
        prob_grads = dot(vb[span, :], grads_t)
        score_grads = (probs.astype(jnp.float32) * (prob_grads - delta)).astype(jnp.bfloat16)
        dv_acc[span, :] += dot(probs, grads)
        dk_acc[span, :] += dot(score_grads, qb[n, pl.ds(base, TILE), :])
        return dot(kt[:, span], score_grads)

    def finish(n, i, base, dq_t):
        gqb[n, pl.ds(base, TILE), :] = (dq_t * ATTN_SCALE).T.astype(jnp.bfloat16)

    await_bytes(qb.at[0], recv.at[2])
    forward(0)
    await_bytes(qb.at[1], recv.at[3])
    forward(1)
    await_bytes(gb.at[0], recv.at[4])

    def backward(j, carry):
        for i in (2 * j, 2 * j + 1):
            base, grads, grads_t, delta = grads_of(0, i)
            finish(0, i, base, part(0, i, base, 0, SPAN, grads, grads_t, delta))
        for i in (2 * j, 2 * j + 1):
            for dx in range(4):
                send_back(gqb.at[0], gq_ref, 2, 0, i, dx, 2)
        return carry

    lax.fori_loop(0, STEPS // 2, backward, 0)
    await_bytes(gb.at[1], recv.at[5])

    for i in range(STEPS):
        dq[i] = part(1, i, i * TILE, 0, WINDOW - i * TILE, *grads_of(1, i)[1:])
    dk_out[...] = (dk_acc[older, :] * ATTN_SCALE).astype(jnp.bfloat16)
    dv_out[...] = dv_acc[older, :].astype(jnp.bfloat16)
    back = []
    for index, (src, dst) in enumerate(((dk_out, dk_in), (dv_out, dv_in))):
        copy = pltpu.make_async_remote_copy(
            src_ref=src, dst_ref=dst, send_sem=ring_send.at[3 + index], recv_sem=ring_recv.at[3 + index],
            device_id=before, device_id_type=MESH,
        )
        pl.when(has_before)(copy.start)
        back.append(copy)

    @pl.when(jnp.logical_not(has_after))
    def _():
        dk_in[...] = jnp.zeros_like(dk_in)
        dv_in[...] = jnp.zeros_like(dv_in)

    for i in range(STEPS):
        base, grads, grads_t, delta = grads_of(1, i)
        first = WINDOW - i * TILE
        finish(1, i, base, dq[i] + part(1, i, base, first, SPAN - first, grads, grads_t, delta))
        for dx in range(4):
            send_back(gqb.at[1], gq_ref, 2, 1, i, dx, 3)

    pl.when(has_after)(back[0].wait_recv)
    gkb[...] = (dk_acc[newer, :] * ATTN_SCALE + dk_in[...].astype(jnp.float32)).astype(jnp.bfloat16)
    for i in range(STEPS):
        for dx in range(4):
            send_back(gkb, gk_ref, 1, 0, i, dx, 4)
    pl.when(has_after)(back[1].wait_recv)
    gvb[...] = (dv_acc[newer, :] + dv_in[...].astype(jnp.float32)).astype(jnp.bfloat16)
    for i in range(STEPS):
        for dx in range(4):
            send_back(gvb, gv_ref, 1, 0, i, dx, 5)

    for copy in ring:
        pl.when(has_after)(copy.wait_send)
    for copy in back:
        pl.when(has_before)(copy.wait_send)
    for _ in range(3):
        await_bytes(seg_ref, send.at[6])
    pl.when(leaves)(functools.partial(await_bytes, seg_ref, send.at[6]))
    for sems in (send, out_send):
        for index in range(6):
            await_bytes(gkb.at[pl.ds(0, 15 * ROWS), :], sems.at[index])
            pl.when(leaves)(functools.partial(await_bytes, gkb.at[pl.ds(0, ROWS), :], sems.at[index]))
    everything = pl.ds(0, KVHEADS * HEAD_DIM)
    for index, out in enumerate((a_ref, a_ref, gq_ref, gq_ref, gk_ref, gv_ref)):
        await_bytes(out.at[:, everything], out_recv.at[index])


def deliver(a_ref, gq_ref, gk_ref, gv_ref, *rest):
    outs, sem = rest[:4], rest[4]
    copies = [
        pltpu.make_async_copy(src, dst, sem.at[n])
        for n, (src, dst) in enumerate(zip((a_ref, gq_ref, gk_ref, gv_ref), outs))
    ]
    for copy in copies:
        copy.start()
    for copy in copies:
        copy.wait()


def body(queries, keys, values, grad_out, segments):
    low = jnp.bfloat16
    shape = jax.ShapeDtypeStruct
    outs = (
        shape(queries.shape, low),
        shape(queries.shape, low),
        shape(keys.shape, low),
        shape(keys.shape, low),
    )
    wide, narrow = queries.shape, keys.shape
    queries, keys, values, grad_out, segments = (
        pltpu.with_memory_space_constraint(a, pltpu.HBM)
        for a in (queries, keys, values, grad_out, segments.reshape(1, TILE))
    )
    results = pl.pallas_call(
        kernel,
        out_shape=outs,
        in_specs=[pl.BlockSpec(memory_space=pltpu.HBM)] * 4 + [pl.BlockSpec(memory_space=pltpu.VMEM)],
        out_specs=[pl.BlockSpec(memory_space=pl.ANY)] * 4,
        scratch_shapes=[
            pltpu.VMEM(wide, low),
            pltpu.VMEM(narrow, low),
            pltpu.VMEM(narrow, low),
            pltpu.VMEM(wide, low),
            pltpu.VMEM((2, WINDOW, HEAD_DIM), low),
            pltpu.VMEM((2 * WINDOW, HEAD_DIM), low),
            pltpu.VMEM((2 * WINDOW, HEAD_DIM), low),
            pltpu.VMEM((2, WINDOW, HEAD_DIM), low),
            pltpu.VMEM((2 * STEPS, 1, TILE), jnp.int32),
            pltpu.VMEM((HEAD_DIM, 2 * WINDOW), low),
            pltpu.VMEM((HEAD_DIM, 2 * WINDOW), low),
            pltpu.VMEM((2, STEPS, SPAN, TILE), low),
            pltpu.VMEM((2, STEPS, HEAD_DIM, TILE), jnp.float32),
            pltpu.VMEM((STEPS, HEAD_DIM, TILE), jnp.float32),
            pltpu.VMEM((STEPS, 1, TILE), jnp.int32),
            pltpu.VMEM((2, WINDOW, HEAD_DIM), low),
            pltpu.VMEM((2, WINDOW, HEAD_DIM), low),
            pltpu.VMEM((2 * WINDOW, HEAD_DIM), jnp.float32),
            pltpu.VMEM((2 * WINDOW, HEAD_DIM), jnp.float32),
            pltpu.VMEM((WINDOW, HEAD_DIM), low),
            pltpu.VMEM((WINDOW, HEAD_DIM), low),
            pltpu.VMEM((WINDOW, HEAD_DIM), low),
            pltpu.VMEM((WINDOW, HEAD_DIM), low),
            pltpu.VMEM((WINDOW, HEAD_DIM), low),
            pltpu.VMEM((WINDOW, HEAD_DIM), low),
            pltpu.SemaphoreType.DMA((4,)),
            pltpu.SemaphoreType.DMA((7,)),
            pltpu.SemaphoreType.DMA((7,)),
            pltpu.SemaphoreType.DMA((5,)),
            pltpu.SemaphoreType.DMA((5,)),
            pltpu.SemaphoreType.DMA((6,)),
            pltpu.SemaphoreType.DMA((6,)),
        ],
        compiler_params=pltpu.CompilerParams(
            collective_id=0, has_side_effects=True, vmem_limit_bytes=48 * 1024 * 1024
        ),
    )(queries, keys, values, grad_out, segments)
    return pl.pallas_call(
        deliver,
        out_shape=outs,
        in_specs=[pl.BlockSpec(memory_space=pltpu.VMEM)] * 4,
        out_specs=[pl.BlockSpec(memory_space=pl.ANY)] * 4,
        scratch_shapes=[pltpu.SemaphoreType.DMA((4,))],
        compiler_params=pltpu.CompilerParams(vmem_limit_bytes=8 * 1024 * 1024),
    )(*results)


def solution(mesh):
    spec = P(("ctx", "head"), None)
    return jax.shard_map(
        body,
        mesh=mesh,
        in_specs=(spec, spec, spec, spec, P("ctx")),
        out_specs=(spec, spec, spec, spec),
        check_vma=False,
    )
```

time: 63.8 us -> 51.1 us (0.80)
  the two profiles are of different devices: /device:TPU:1 before, /device:TPU:121 now
where the time goes in v2:
time: 51.1 us; the launch traced here: 51 us
  Pallas kernels  50.4 us (99%)
  between operations  0.64 us (1%)
    pallas_call x1, Pallas kernels, body(): pl.pallas_call(kernel, out_shape=outs, in_specs=[pl.BlockSpec(memory_spac...  49.2 us
    pallas_call x1, Pallas kernels, body(): pl.pallas_call(deliver, out_shape=outs, in_specs=[pl.BlockSpec(memory_spa...  1.17 us

profile of v2, /device:TPU:121, one launch (start us, length us, event | category | flops | bytes accessed | tf_op | source)
XLA Modules:
  0.0 51.0 jit_solution(15314594971902191635)
XLA Ops:
  0.6 49.2 %shard_map.84 = (bf16[64,4096]{1,0:T(8,128)(2,1)S(1)}, bf16[64,4096]{1,0:T(8,128)(2,1)S(1)}, bf16[64,2048]{1,0:T(8,128)(2,1)S(1)}, bf16[64,2048]{1,0:T(8,128)(2,1)S(1)}) custom-call(bf16[64,4096]{1,0:T(8,128)(2,1)} %q_ref.1, bf16[64,2048]{1,0:T(8,128)(2,1)} %k_ref.1, bf16[64,2048]{1,0:T(8,128)(2,1)} %v_ref.1, bf16[64,4096]{1,0:T(8,128)(2,1)} %g_ref.1, ...), custom_call_target="tpu_custom_call" | custom-call | tf_op jit(solution)/shard_map/pallas_call | solution.py:335
  49.8 1.2 %shard_map.85 = (bf16[64,4096]{1,0:T(8,128)(2,1)}, bf16[64,4096]{1,0:T(8,128)(2,1)}, bf16[64,2048]{1,0:T(8,128)(2,1)}, bf16[64,2048]{1,0:T(8,128)(2,1)}) custom-call(bf16[64,4096]{1,0:T(8,128)(2,1)S(1)} %get-tuple-element.8.a_ref, bf16[64,4096]{1,0:T(8,128)(2,1)S(1)} %get-tuple-element.9.gq_ref, bf16[64,2048]{1,0:T(8,128)(2,1)S(1)} %get-tuple-element.10.gk_ref, ...), custom_call_target="tpu_custom_call" | custom-call | tf_op jit(solution)/shard_map/pallas_call | solution.py:378

commit v3 on v2

--- a/solution.py
+++ b/solution.py
@@ -23,6 +23,8 @@
 STEPS = WINDOW // TILE
 SPAN = WINDOW + TILE
 HIDDEN = -1e30
+APART = 2.0**17
+WIDE = 2 * HEAD_DIM
 
 
 def dot(a, b, dims=((1,), (0,))):
@@ -38,7 +40,7 @@
     a_ref, gq_ref, gk_ref, gv_ref,
     q_own, k_own, v_own, g_own,
     qb, kb, vb, gb, segb,
-    kt, vt, pb, ot, dq, lo_buf, ab, gqb, dk_acc, dv_acc, dk_out, dv_out, dk_in, dv_in, gkb, gvb,
+    kt, vt, sb, pb, ot, inv, dq, ab, gqb, dk_acc, dv_acc, dk_out, dv_out, dk_in, dv_in, gkb, gvb,
     load, send, recv, ring_send, ring_recv, out_send, out_recv,
 ):
     ctx, x = lax.axis_index("ctx"), lax.axis_index("head")
@@ -79,7 +81,7 @@
 
     @pl.when(jnp.logical_not(has_before))
     def _():
-        kb[older, :] = jnp.zeros((WINDOW, HEAD_DIM), kb.dtype)
+        kb[older, slice(0, HEAD_DIM)] = jnp.zeros((WINDOW, HEAD_DIM), kb.dtype)
         vb[older, :] = jnp.zeros((WINDOW, HEAD_DIM), vb.dtype)
         segb[pl.ds(0, STEPS)] = jnp.full((STEPS, 1, TILE), -1, segb.dtype)
 
@@ -103,7 +105,7 @@
             pl.when(jnp.logical_not(local))(far)
 
     offsets = [(dx, dy) for dx in range(4) for dy in range(4)]
-    offsets = sorted(offsets, key=lambda o: min(o[0], 4 - o[0]) + min(o[1], 4 - o[1]))
+    offsets = sorted(offsets, key=lambda o: -min(o[0], 4 - o[0]) - min(o[1], 4 - o[1]))
     own_rows = pl.ds(pl.multiple_of(slot * ROWS, ROWS), ROWS)
     own_rows2 = pl.ds(pl.multiple_of(WINDOW + slot * ROWS, ROWS), ROWS)
     for dy in range(4):
@@ -112,11 +114,12 @@
             seg_ref, segb.at[STEPS + (y % 2) * 2 + core], send.at[6], recv.at[6],
             where, stays if dy == 0 else None,
         )
+    head_part, doc_part = pl.ds(0, HEAD_DIM), pl.ds(HEAD_DIM, HEAD_DIM)
     streams = (
-        (k_own, kb, own_rows2, 1, 0, 0),
+        (k_own, kb.at[:, head_part], own_rows2, 1, 0, 0),
         (v_own, vb, own_rows2, 1, 0, 1),
-        (q_own, qb.at[0], own_rows, 2, 0, 2),
-        (q_own, qb.at[1], own_rows, 2, 1, None),
+        (q_own, qb.at[0, :, head_part], own_rows, 2, 0, 2),
+        (q_own, qb.at[1, :, head_part], own_rows, 2, 1, None),
         (g_own, gb.at[0], own_rows, 2, 0, 3),
         (g_own, gb.at[1], own_rows, 2, 1, None),
     )
@@ -139,7 +142,7 @@
     for index, (buf, here, there) in enumerate(
         (
             (segb, pl.ds(STEPS, STEPS), pl.ds(0, STEPS)),
-            (kb, newer, older),
+            (kb.at[:, head_part], newer, older),
             (vb, newer, older),
         )
     ):
@@ -152,106 +155,115 @@
         pl.when(has_after)(copy.start)
         ring.append(copy)
 
-    kt[:, newer] = kb[newer, :].T
+    kind = lax.broadcasted_iota(jnp.int32, (HEAD_DIM, TILE), 0)
+
+    def documents(r):
+        number = segb[r]
+        number = jnp.where(number < 0, DOCS, number)
+        return jnp.where(kind == number, 1.0, 0.0).T
+
+    for r in range(STEPS):
+        hot = documents(STEPS + r)
+        kb[pl.ds(WINDOW + r * TILE, TILE), doc_part] = hot.astype(kb.dtype)
+        apart = ((hot - 1.0) * APART).astype(qb.dtype)
+        for n in range(2):
+            qb[n, pl.ds(r * TILE, TILE), doc_part] = apart
+    kt[:, newer] = kb[newer, head_part].T
     vt[:, newer] = vb[newer, :].T
     dk_acc[...] = jnp.zeros_like(dk_acc)
     dv_acc[...] = jnp.zeros_like(dv_acc)
     pl.when(has_before)(ring[0].wait_recv)
-    rows = [segb[r].astype(jnp.float32) for r in range(2 * STEPS)]
-    all_rows = jnp.concatenate(rows, axis=0)
-    starts = [
-        jnp.sum(
-            jnp.sum((all_rows < d).astype(jnp.float32), axis=0, keepdims=True), axis=1, keepdims=True
-        )
-        for d in range(DOCS)
-    ]
-    lane = lax.broadcasted_iota(jnp.int32, (1, TILE), 1).astype(jnp.float32)
-    for i in range(STEPS):
-        row = rows[STEPS + i]
-        first = lane + (i * TILE + 1.0)
-        for d in range(DOCS):
-            first = jnp.maximum(first, jnp.where(row >= d, starts[d], 0.0))
-        lo_buf[i] = (first - i * TILE).astype(jnp.int32)
+    for r in range(STEPS):
+        kb[pl.ds(r * TILE, TILE), doc_part] = documents(r).astype(kb.dtype)
     pl.when(has_before)(ring[1].wait_recv)
-    kt[:, older] = kb[older, :].T
+    kt[:, older] = kb[older, head_part].T
     pl.when(has_before)(ring[2].wait_recv)
     vt[:, older] = vb[older, :].T
 
-    key_index = lax.broadcasted_iota(jnp.int32, (SPAN, TILE), 0)
-    last_key = WINDOW + lax.broadcasted_iota(jnp.int32, (1, TILE), 1)
-
-    def send_back(buf, out, per, n, i, dx, index):
-        yy, c = i // 2, i % 2
-        tx = (x + dx) % 4
-        ty = core * 2 + yy
-        where = ((z * 4 + ty) * 2 + c, tx)
-        ship(
-            buf.at[pl.ds(pl.multiple_of((i * 4 + tx) * ROWS, ROWS), ROWS), :],
-            out.at[:, pl.ds(pl.multiple_of((group * per + n) * HEAD_DIM, HEAD_DIM), HEAD_DIM)],
-            out_send.at[index],
-            out_recv.at[index],
-            where,
-            ((ty == y) & (c == core)) if dx == 0 else None,
-        )
+    key_at = lax.broadcasted_iota(jnp.int32, (TILE, TILE), 0)
+    query_at = lax.broadcasted_iota(jnp.int32, (TILE, TILE), 1)
+
+    def send_back(buf, out, per, n, index):
+        column = pl.ds(pl.multiple_of((group * per + n) * HEAD_DIM, HEAD_DIM), HEAD_DIM)
+        for dx in (2, 1, 3, 0):
+            for turn in range(2):
+                for c in range(2):
+                    yy = (y + turn) % 2
+                    tx, ty = (x + dx) % 4, core * 2 + yy
+                    ship(
+                        buf.at[pl.ds(pl.multiple_of(((yy * 2 + c) * 4 + tx) * ROWS, ROWS), ROWS), :],
+                        out.at[:, column],
+                        out_send.at[index],
+                        out_recv.at[index],
+                        ((z * 4 + ty) * 2 + c, tx),
+                        ((ty == y) & (c == core)) if dx == 0 and turn == 0 else None,
+                    )
 
     def forward(n):
-        def step(j, carry):
-            for i in (2 * j, 2 * j + 1):
-                base = pl.multiple_of(i * TILE, TILE)
-                seen = (key_index >= lo_buf[i]) & (key_index <= last_key)
-                scores = dot(kb[pl.ds(base, SPAN), :], qb[n, pl.ds(base, TILE), :], ((1,), (1,)))
-                scores = jnp.where(seen, scores, HIDDEN)
-                top = jnp.max(scores, axis=0, keepdims=True)
-                weights = jnp.exp2(scores * EXP2_SCALE - top * EXP2_SCALE)
-                total = jnp.sum(weights, axis=0, keepdims=True)
-                probs = (weights * (1.0 / total)).astype(jnp.bfloat16)
-                pb[n, i] = probs
-                out_t = dot(vt[:, pl.ds(base, SPAN)], probs)
-                ot[n, i] = out_t
-                ab[n, pl.ds(base, TILE), :] = out_t.T.astype(jnp.bfloat16)
-            for i in (2 * j, 2 * j + 1):
-                for dx in range(4):
-                    send_back(ab.at[n], a_ref, 2, n, i, dx, n)
-            return carry
-
-        lax.fori_loop(0, STEPS // 2, step, 0)
+        def score(i, t):
+            rows = pl.ds(t * TILE, TILE)
+            scores = dot(
+                kb[pl.ds((i + t) * TILE, TILE), :], qb[n, pl.ds(i * TILE, TILE), :], ((1,), (1,))
+            )
+            if t == 0:
+                scores = jnp.where(key_at > query_at, scores, HIDDEN)
+            if t == STEPS:
+                scores = jnp.where(key_at <= query_at, scores, HIDDEN)
+            sb[i % 2, rows, :] = scores
+            return jnp.max(scores, axis=0, keepdims=True)
+
+        tops = [score(0, t) for t in range(STEPS + 1)]
+        for i in range(STEPS):
+            top, tops, total = functools.reduce(jnp.maximum, tops), [], 0.0
+            for t in range(STEPS + 1):
+                rows = pl.ds(t * TILE, TILE)
+                weights = jnp.exp2((sb[i % 2, rows, :] - top) * EXP2_SCALE)
+                total = total + jnp.sum(weights, axis=0, keepdims=True)
+                pb[n, i, rows, :] = weights.astype(jnp.bfloat16)
+                if i + 1 < STEPS:
+                    tops.append(score(i + 1, t))
+            scale = 1.0 / total
+            inv[n, i] = scale
+            out_t = (dot(vt[:, pl.ds(i * TILE, SPAN)], pb[n, i]) * scale).astype(jnp.bfloat16)
+            ot[n, i] = out_t
+            ab[n, pl.ds(i * TILE, TILE), :] = out_t.T
+        send_back(ab.at[n], a_ref, 2, n, n)
 
     def grads_of(n, i):
         base = pl.multiple_of(i * TILE, TILE)
-        grads = gb[n, pl.ds(base, TILE), :]
-        grads_t = grads.T
-        low = ot[n, i].astype(jnp.bfloat16).astype(jnp.float32)
-        delta = jnp.sum(low * grads_t.astype(jnp.float32), axis=0, keepdims=True)
-        return base, grads, grads_t, delta
-
-    def part(n, i, base, first, count, grads, grads_t, delta):
+        grads_t = gb[n, pl.ds(base, TILE), :].T.astype(jnp.float32) * inv[n, i]
+        grads_t = grads_t.astype(jnp.bfloat16)
+        delta = jnp.sum(
+            ot[n, i].astype(jnp.float32) * grads_t.astype(jnp.float32), axis=0, keepdims=True
+        )
+        return base, grads_t, delta
+
+    def part(n, i, base, first, count, grads_t, delta):
         span = pl.ds(pl.multiple_of(base + first, TILE), count)
-        probs = pb[n, i, first : first + count, :]
+        weights = pb[n, i, first : first + count, :]
         prob_grads = dot(vb[span, :], grads_t)
-        score_grads = (probs.astype(jnp.float32) * (prob_grads - delta)).astype(jnp.bfloat16)
-        dv_acc[span, :] += dot(probs, grads)
-        dk_acc[span, :] += dot(score_grads, qb[n, pl.ds(base, TILE), :])
+        score_grads = (weights.astype(jnp.float32) * (prob_grads - delta)).astype(jnp.bfloat16)
+        dv_acc[span, :] += dot(weights, grads_t, ((1,), (1,)))
+        dk_acc[span, :] += dot(score_grads, qb[n, pl.ds(base, TILE), head_part])
         return dot(kt[:, span], score_grads)
 
     def finish(n, i, base, dq_t):
         gqb[n, pl.ds(base, TILE), :] = (dq_t * ATTN_SCALE).T.astype(jnp.bfloat16)
 
-    await_bytes(qb.at[0], recv.at[2])
+    await_bytes(qb.at[0, :, head_part], recv.at[2])
     forward(0)
-    await_bytes(qb.at[1], recv.at[3])
+    await_bytes(qb.at[1, :, head_part], recv.at[3])
     forward(1)
     await_bytes(gb.at[0], recv.at[4])
 
     def backward(j, carry):
         for i in (2 * j, 2 * j + 1):
-            base, grads, grads_t, delta = grads_of(0, i)
-            finish(0, i, base, part(0, i, base, 0, SPAN, grads, grads_t, delta))
-        for i in (2 * j, 2 * j + 1):
-            for dx in range(4):
-                send_back(gqb.at[0], gq_ref, 2, 0, i, dx, 2)
+            base, grads_t, delta = grads_of(0, i)
+            finish(0, i, base, part(0, i, base, 0, SPAN, grads_t, delta))
         return carry
 
     lax.fori_loop(0, STEPS // 2, backward, 0)
+    send_back(gqb.at[0], gq_ref, 2, 0, 2)
     await_bytes(gb.at[1], recv.at[5])
 
     for i in range(STEPS):
@@ -273,22 +285,17 @@
         dv_in[...] = jnp.zeros_like(dv_in)
 
     for i in range(STEPS):
-        base, grads, grads_t, delta = grads_of(1, i)
+        base, grads_t, delta = grads_of(1, i)
         first = WINDOW - i * TILE
-        finish(1, i, base, dq[i] + part(1, i, base, first, SPAN - first, grads, grads_t, delta))
-        for dx in range(4):
-            send_back(gqb.at[1], gq_ref, 2, 1, i, dx, 3)
+        finish(1, i, base, dq[i] + part(1, i, base, first, SPAN - first, grads_t, delta))
+    send_back(gqb.at[1], gq_ref, 2, 1, 3)
 
     pl.when(has_after)(back[0].wait_recv)
     gkb[...] = (dk_acc[newer, :] * ATTN_SCALE + dk_in[...].astype(jnp.float32)).astype(jnp.bfloat16)
-    for i in range(STEPS):
-        for dx in range(4):
-            send_back(gkb, gk_ref, 1, 0, i, dx, 4)
+    send_back(gkb, gk_ref, 1, 0, 4)
     pl.when(has_after)(back[1].wait_recv)
     gvb[...] = (dv_acc[newer, :] + dv_in[...].astype(jnp.float32)).astype(jnp.bfloat16)
-    for i in range(STEPS):
-        for dx in range(4):
-            send_back(gvb, gv_ref, 1, 0, i, dx, 5)
+    send_back(gvb, gv_ref, 1, 0, 5)
 
     for copy in ring:
         pl.when(has_after)(copy.wait_send)
@@ -342,17 +349,18 @@
             pltpu.VMEM(narrow, low),
             pltpu.VMEM(narrow, low),
             pltpu.VMEM(wide, low),
-            pltpu.VMEM((2, WINDOW, HEAD_DIM), low),
-            pltpu.VMEM((2 * WINDOW, HEAD_DIM), low),
+            pltpu.VMEM((2, WINDOW, WIDE), low),
+            pltpu.VMEM((2 * WINDOW, WIDE), low),
             pltpu.VMEM((2 * WINDOW, HEAD_DIM), low),
             pltpu.VMEM((2, WINDOW, HEAD_DIM), low),
             pltpu.VMEM((2 * STEPS, 1, TILE), jnp.int32),
             pltpu.VMEM((HEAD_DIM, 2 * WINDOW), low),
             pltpu.VMEM((HEAD_DIM, 2 * WINDOW), low),
+            pltpu.VMEM((2, SPAN, TILE), jnp.float32),
             pltpu.VMEM((2, STEPS, SPAN, TILE), low),
-            pltpu.VMEM((2, STEPS, HEAD_DIM, TILE), jnp.float32),
+            pltpu.VMEM((2, STEPS, HEAD_DIM, TILE), low),
+            pltpu.VMEM((2, STEPS, 1, TILE), jnp.float32),
             pltpu.VMEM((STEPS, HEAD_DIM, TILE), jnp.float32),
-            pltpu.VMEM((STEPS, 1, TILE), jnp.int32),
             pltpu.VMEM((2, WINDOW, HEAD_DIM), low),
             pltpu.VMEM((2, WINDOW, HEAD_DIM), low),
             pltpu.VMEM((2 * WINDOW, HEAD_DIM), jnp.float32),

time: 51.1 us -> 47.6 us (0.932)
  the two profiles are of different devices: /device:TPU:121 before, /device:TPU:113 now
where the time goes in v3:
time: 47.6 us; the launch traced here: 47.5 us
  Pallas kernels  46.9 us (99%)
  between operations  0.64 us (1%)
    pallas_call x1, Pallas kernels, body(): pl.pallas_call(kernel, out_shape=outs, in_specs=[pl.BlockSpec(memory_spac...  45.7 us
    pallas_call x1, Pallas kernels, body(): pl.pallas_call(deliver, out_shape=outs, in_specs=[pl.BlockSpec(memory_spa...  1.17 us

profile of v3, /device:TPU:113, one launch (start us, length us, event | category | flops | bytes accessed | tf_op | source)
XLA Modules:
  0.0 47.5 jit_solution(15396682873547038813)
XLA Ops:
  0.6 45.7 %shard_map.84 = (bf16[64,4096]{1,0:T(8,128)(2,1)S(1)}, bf16[64,4096]{1,0:T(8,128)(2,1)S(1)}, bf16[64,2048]{1,0:T(8,128)(2,1)S(1)}, bf16[64,2048]{1,0:T(8,128)(2,1)S(1)}) custom-call(bf16[64,4096]{1,0:T(8,128)(2,1)} %q_ref.1, bf16[64,2048]{1,0:T(8,128)(2,1)} %k_ref.1, bf16[64,2048]{1,0:T(8,128)(2,1)} %v_ref.1, bf16[64,4096]{1,0:T(8,128)(2,1)} %g_ref.1, ...), custom_call_target="tpu_custom_call" | custom-call | tf_op jit(solution)/shard_map/pallas_call | solution.py:342
  46.3 1.2 %shard_map.85 = (bf16[64,4096]{1,0:T(8,128)(2,1)}, bf16[64,4096]{1,0:T(8,128)(2,1)}, bf16[64,2048]{1,0:T(8,128)(2,1)}, bf16[64,2048]{1,0:T(8,128)(2,1)}) custom-call(bf16[64,4096]{1,0:T(8,128)(2,1)S(1)} %get-tuple-element.8.a_ref, bf16[64,4096]{1,0:T(8,128)(2,1)S(1)} %get-tuple-element.9.gq_ref, bf16[64,2048]{1,0:T(8,128)(2,1)S(1)} %get-tuple-element.10.gk_ref, ...), custom_call_target="tpu_custom_call" | custom-call | tf_op jit(solution)/shard_map/pallas_call | solution.py:386

commit v4 on v3

--- a/solution.py
+++ b/solution.py
@@ -38,7 +38,7 @@
 def kernel(
     q_ref, k_ref, v_ref, g_ref, seg_ref,
     a_ref, gq_ref, gk_ref, gv_ref,
-    q_own, k_own, v_own, g_own,
+    q_own, k_own, v_own, g_own, seg_own,
     qb, kb, vb, gb, segb,
     kt, vt, sb, pb, ot, inv, dq, ab, gqb, dk_acc, dv_acc, dk_out, dv_out, dk_in, dv_in, gkb, gvb,
     load, send, recv, ring_send, ring_recv, out_send, out_recv,
@@ -72,7 +72,13 @@
     loads = [
         pltpu.make_async_copy(src, dst, load.at[n])
         for n, (src, dst) in enumerate(
-            ((k_ref, k_own), (v_ref, v_own), (q_ref, q_own), (g_ref, g_own))
+            (
+                (k_ref, k_own),
+                (v_ref, v_own),
+                (q_ref, q_own),
+                (g_ref, g_own),
+                (seg_ref, seg_own),
+            )
         )
     ]
     for copy in loads:
@@ -108,10 +114,11 @@
     offsets = sorted(offsets, key=lambda o: -min(o[0], 4 - o[0]) - min(o[1], 4 - o[1]))
     own_rows = pl.ds(pl.multiple_of(slot * ROWS, ROWS), ROWS)
     own_rows2 = pl.ds(pl.multiple_of(WINDOW + slot * ROWS, ROWS), ROWS)
+    loads[4].wait()
     for dy in range(4):
         where, _ = target(0, dy)
         ship(
-            seg_ref, segb.at[STEPS + (y % 2) * 2 + core], send.at[6], recv.at[6],
+            seg_own, segb.at[STEPS + (y % 2) * 2 + core], send.at[6], recv.at[6],
             where, stays if dy == 0 else None,
         )
     head_part, doc_part = pl.ds(0, HEAD_DIM), pl.ds(HEAD_DIM, HEAD_DIM)
@@ -177,27 +184,27 @@
         kb[pl.ds(r * TILE, TILE), doc_part] = documents(r).astype(kb.dtype)
     pl.when(has_before)(ring[1].wait_recv)
     kt[:, older] = kb[older, head_part].T
-    pl.when(has_before)(ring[2].wait_recv)
-    vt[:, older] = vb[older, :].T
 
     key_at = lax.broadcasted_iota(jnp.int32, (TILE, TILE), 0)
     query_at = lax.broadcasted_iota(jnp.int32, (TILE, TILE), 1)
 
+    def send_block(buf, out, per, n, index, yy, c, dx, maybe_here):
+        tx, ty = (x + dx) % 4, core * 2 + yy
+        ship(
+            buf.at[pl.ds(pl.multiple_of(((yy * 2 + c) * 4 + tx) * ROWS, ROWS), ROWS), :],
+            out.at[:, pl.ds(pl.multiple_of((group * per + n) * HEAD_DIM, HEAD_DIM), HEAD_DIM)],
+            out_send.at[index],
+            out_recv.at[index],
+            ((z * 4 + ty) * 2 + c, tx),
+            ((ty == y) & (c == core)) if maybe_here else None,
+        )
+
     def send_back(buf, out, per, n, index):
-        column = pl.ds(pl.multiple_of((group * per + n) * HEAD_DIM, HEAD_DIM), HEAD_DIM)
         for dx in (2, 1, 3, 0):
             for turn in range(2):
                 for c in range(2):
-                    yy = (y + turn) % 2
-                    tx, ty = (x + dx) % 4, core * 2 + yy
-                    ship(
-                        buf.at[pl.ds(pl.multiple_of(((yy * 2 + c) * 4 + tx) * ROWS, ROWS), ROWS), :],
-                        out.at[:, column],
-                        out_send.at[index],
-                        out_recv.at[index],
-                        ((z * 4 + ty) * 2 + c, tx),
-                        ((ty == y) & (c == core)) if dx == 0 and turn == 0 else None,
-                    )
+                    here = dx == 0 and turn == 0
+                    send_block(buf, out, per, n, index, (y + turn) % 2, c, dx, here)
 
     def forward(n):
         def score(i, t):
@@ -224,6 +231,9 @@
                     tops.append(score(i + 1, t))
             scale = 1.0 / total
             inv[n, i] = scale
+            if n == 0 and i == 0:
+                pl.when(has_before)(ring[2].wait_recv)
+                vt[:, older] = vb[older, :].T
             out_t = (dot(vt[:, pl.ds(i * TILE, SPAN)], pb[n, i]) * scale).astype(jnp.bfloat16)
             ot[n, i] = out_t
             ab[n, pl.ds(i * TILE, TILE), :] = out_t.T
@@ -266,18 +276,24 @@
     send_back(gqb.at[0], gq_ref, 2, 0, 2)
     await_bytes(gb.at[1], recv.at[5])
 
+    def returned(b, index, src, dst):
+        rows = pl.ds(pl.multiple_of(b * TILE, TILE), TILE)
+        return pltpu.make_async_remote_copy(
+            src_ref=src.at[rows, :], dst_ref=dst.at[rows, :],
+            send_sem=ring_send.at[3 + index * STEPS + b], recv_sem=ring_recv.at[3 + index * STEPS + b],
+            device_id=before, device_id_type=MESH,
+        )
+
     for i in range(STEPS):
         dq[i] = part(1, i, i * TILE, 0, WINDOW - i * TILE, *grads_of(1, i)[1:])
-    dk_out[...] = (dk_acc[older, :] * ATTN_SCALE).astype(jnp.bfloat16)
-    dv_out[...] = dv_acc[older, :].astype(jnp.bfloat16)
-    back = []
-    for index, (src, dst) in enumerate(((dk_out, dk_in), (dv_out, dv_in))):
-        copy = pltpu.make_async_remote_copy(
-            src_ref=src, dst_ref=dst, send_sem=ring_send.at[3 + index], recv_sem=ring_recv.at[3 + index],
-            device_id=before, device_id_type=MESH,
-        )
-        pl.when(has_before)(copy.start)
-        back.append(copy)
+        rows = pl.ds(i * TILE, TILE)
+        dk_out[rows, :] = (dk_acc[rows, :] * ATTN_SCALE).astype(jnp.bfloat16)
+        dv_out[rows, :] = dv_acc[rows, :].astype(jnp.bfloat16)
+
+        @pl.when(has_before)
+        def _():
+            returned(i, 0, dk_out, dk_in).start()
+            returned(i, 1, dv_out, dv_in).start()
 
     @pl.when(jnp.logical_not(has_after))
     def _():
@@ -290,20 +306,39 @@
         finish(1, i, base, dq[i] + part(1, i, base, first, SPAN - first, grads_t, delta))
     send_back(gqb.at[1], gq_ref, 2, 1, 3)
 
-    pl.when(has_after)(back[0].wait_recv)
-    gkb[...] = (dk_acc[newer, :] * ATTN_SCALE + dk_in[...].astype(jnp.float32)).astype(jnp.bfloat16)
-    send_back(gkb, gk_ref, 1, 0, 4)
-    pl.when(has_after)(back[1].wait_recv)
-    gvb[...] = (dv_acc[newer, :] + dv_in[...].astype(jnp.float32)).astype(jnp.bfloat16)
-    send_back(gvb, gv_ref, 1, 0, 5)
+    first_block = 0 * y
+
+    def settle(step, carry):
+        b = (step + first_block) % STEPS
+        rows = pl.ds(pl.multiple_of(b * TILE, TILE), TILE)
+        rows_acc = pl.ds(pl.multiple_of(WINDOW + b * TILE, TILE), TILE)
+        for index, (acc, factor, src, came, buf, out) in enumerate(
+            (
+                (dk_acc, ATTN_SCALE, dk_out, dk_in, gkb, gk_ref),
+                (dv_acc, 1.0, dv_out, dv_in, gvb, gv_ref),
+            )
+        ):
+            pl.when(has_after)(returned(b, index, src, came).wait_recv)
+            total = acc[rows_acc, :] * factor + came[rows, :].astype(jnp.float32)
+            buf[rows, :] = total.astype(jnp.bfloat16)
+            for dx in (2, 1, 3, 0):
+                send_block(buf, out, 1, 0, 4 + index, b // 2, b % 2, dx, dx == 0)
+        return carry
+
+    lax.fori_loop(0, STEPS, settle, 0)
 
     for copy in ring:
         pl.when(has_after)(copy.wait_send)
-    for copy in back:
-        pl.when(has_before)(copy.wait_send)
+
+    @pl.when(has_before)
+    def _():
+        for b in range(STEPS):
+            returned(b, 0, dk_out, dk_in).wait_send()
+            returned(b, 1, dv_out, dv_in).wait_send()
+
     for _ in range(3):
-        await_bytes(seg_ref, send.at[6])
-    pl.when(leaves)(functools.partial(await_bytes, seg_ref, send.at[6]))
+        await_bytes(seg_own, send.at[6])
+    pl.when(leaves)(functools.partial(await_bytes, seg_own, send.at[6]))
     for sems in (send, out_send):
         for index in range(6):
             await_bytes(gkb.at[pl.ds(0, 15 * ROWS), :], sems.at[index])
@@ -342,13 +377,14 @@
     results = pl.pallas_call(
         kernel,
         out_shape=outs,
-        in_specs=[pl.BlockSpec(memory_space=pltpu.HBM)] * 4 + [pl.BlockSpec(memory_space=pltpu.VMEM)],
+        in_specs=[pl.BlockSpec(memory_space=pltpu.HBM)] * 5,
         out_specs=[pl.BlockSpec(memory_space=pl.ANY)] * 4,
         scratch_shapes=[
             pltpu.VMEM(wide, low),
             pltpu.VMEM(narrow, low),
             pltpu.VMEM(narrow, low),
             pltpu.VMEM(wide, low),
+            pltpu.VMEM((1, TILE), jnp.int32),
             pltpu.VMEM((2, WINDOW, WIDE), low),
             pltpu.VMEM((2 * WINDOW, WIDE), low),
             pltpu.VMEM((2 * WINDOW, HEAD_DIM), low),
@@ -371,11 +407,11 @@
             pltpu.VMEM((WINDOW, HEAD_DIM), low),
             pltpu.VMEM((WINDOW, HEAD_DIM), low),
             pltpu.VMEM((WINDOW, HEAD_DIM), low),
-            pltpu.SemaphoreType.DMA((4,)),
+            pltpu.SemaphoreType.DMA((5,)),
             pltpu.SemaphoreType.DMA((7,)),
             pltpu.SemaphoreType.DMA((7,)),
-            pltpu.SemaphoreType.DMA((5,)),
-            pltpu.SemaphoreType.DMA((5,)),
+            pltpu.SemaphoreType.DMA((11,)),
+            pltpu.SemaphoreType.DMA((11,)),
             pltpu.SemaphoreType.DMA((6,)),
             pltpu.SemaphoreType.DMA((6,)),
         ],

time: 47.6 us -> 46 us (0.966)
  the two profiles are of different devices: /device:TPU:113 before, /device:TPU:1 now
where the time goes in v4:
time: 46 us; the launch traced here: 45.9 us
  Pallas kernels  45.2 us (98%)
  between operations  0.64 us (1%)
    pallas_call x1, Pallas kernels, body(): pl.pallas_call(kernel, out_shape=outs, in_specs=[pl.BlockSpec(memory_spac...  44.1 us
    pallas_call x1, Pallas kernels, body(): pl.pallas_call(deliver, out_shape=outs, in_specs=[pl.BlockSpec(memory_spa...  1.17 us

profile of v4, /device:TPU:1, one launch (start us, length us, event | category | flops | bytes accessed | tf_op | source)
XLA Modules:
  0.0 45.9 jit_solution(1464264180166244956)
XLA Ops:
  0.6 44.1 %shard_map.84 = (bf16[64,4096]{1,0:T(8,128)(2,1)S(1)}, bf16[64,4096]{1,0:T(8,128)(2,1)S(1)}, bf16[64,2048]{1,0:T(8,128)(2,1)S(1)}, bf16[64,2048]{1,0:T(8,128)(2,1)S(1)}) custom-call(bf16[64,4096]{1,0:T(8,128)(2,1)} %q_ref.1, bf16[64,2048]{1,0:T(8,128)(2,1)} %k_ref.1, bf16[64,2048]{1,0:T(8,128)(2,1)} %v_ref.1, bf16[64,4096]{1,0:T(8,128)(2,1)} %g_ref.1, ...), custom_call_target="tpu_custom_call" | custom-call | tf_op jit(solution)/shard_map/pallas_call | solution.py:377
  44.7 1.2 %shard_map.85 = (bf16[64,4096]{1,0:T(8,128)(2,1)}, bf16[64,4096]{1,0:T(8,128)(2,1)}, bf16[64,2048]{1,0:T(8,128)(2,1)}, bf16[64,2048]{1,0:T(8,128)(2,1)}) custom-call(bf16[64,4096]{1,0:T(8,128)(2,1)S(1)} %get-tuple-element.8.a_ref, bf16[64,4096]{1,0:T(8,128)(2,1)S(1)} %get-tuple-element.9.gq_ref, bf16[64,2048]{1,0:T(8,128)(2,1)S(1)} %get-tuple-element.10.gk_ref, ...), custom_call_target="tpu_custom_call" | custom-call | tf_op jit(solution)/shard_map/pallas_call | solution.py:422

commit v5 on v4

--- a/solution.py
+++ b/solution.py
@@ -304,14 +304,12 @@
         base, grads_t, delta = grads_of(1, i)
         first = WINDOW - i * TILE
         finish(1, i, base, dq[i] + part(1, i, base, first, SPAN - first, grads_t, delta))
-    send_back(gqb.at[1], gq_ref, 2, 1, 3)
-
-    first_block = 0 * y
-
-    def settle(step, carry):
-        b = (step + first_block) % STEPS
-        rows = pl.ds(pl.multiple_of(b * TILE, TILE), TILE)
-        rows_acc = pl.ds(pl.multiple_of(WINDOW + b * TILE, TILE), TILE)
+        for dx in (2, 1, 3, 0):
+            send_block(gqb.at[1], gq_ref, 2, 1, 3, i // 2, i % 2, dx, dx == 0)
+
+    for b in range(STEPS):
+        rows = pl.ds(b * TILE, TILE)
+        rows_acc = pl.ds(WINDOW + b * TILE, TILE)
         for index, (acc, factor, src, came, buf, out) in enumerate(
             (
                 (dk_acc, ATTN_SCALE, dk_out, dk_in, gkb, gk_ref),
@@ -323,9 +321,6 @@
             buf[rows, :] = total.astype(jnp.bfloat16)
             for dx in (2, 1, 3, 0):
                 send_block(buf, out, 1, 0, 4 + index, b // 2, b % 2, dx, dx == 0)
-        return carry
-
-    lax.fori_loop(0, STEPS, settle, 0)
 
     for copy in ring:
         pl.when(has_after)(copy.wait_send)

time: 46 us -> 45.6 us (level)
  no operation moved by 1% of the time
where the time goes in v5:
time: 45.6 us; the launch traced here: 45.5 us
  Pallas kernels  44.8 us (98%)
  between operations  0.64 us (1%)
    pallas_call x1, Pallas kernels, body(): pl.pallas_call(kernel, out_shape=outs, in_specs=[pl.BlockSpec(memory_spac...  43.7 us
    pallas_call x1, Pallas kernels, body(): pl.pallas_call(deliver, out_shape=outs, in_specs=[pl.BlockSpec(memory_spa...  1.17 us

profile of v5, /device:TPU:1, one launch (start us, length us, event | category | flops | bytes accessed | tf_op | source)
XLA Modules:
  0.0 45.5 jit_solution(17503660446103321604)
XLA Ops:
  0.6 43.7 %shard_map.84 = (bf16[64,4096]{1,0:T(8,128)(2,1)S(1)}, bf16[64,4096]{1,0:T(8,128)(2,1)S(1)}, bf16[64,2048]{1,0:T(8,128)(2,1)S(1)}, bf16[64,2048]{1,0:T(8,128)(2,1)S(1)}) custom-call(bf16[64,4096]{1,0:T(8,128)(2,1)} %q_ref.1, bf16[64,2048]{1,0:T(8,128)(2,1)} %k_ref.1, bf16[64,2048]{1,0:T(8,128)(2,1)} %v_ref.1, bf16[64,4096]{1,0:T(8,128)(2,1)} %g_ref.1, ...), custom_call_target="tpu_custom_call" | custom-call | tf_op jit(solution)/shard_map/pallas_call | solution.py:372
  44.3 1.2 %shard_map.85 = (bf16[64,4096]{1,0:T(8,128)(2,1)}, bf16[64,4096]{1,0:T(8,128)(2,1)}, bf16[64,2048]{1,0:T(8,128)(2,1)}, bf16[64,2048]{1,0:T(8,128)(2,1)}) custom-call(bf16[64,4096]{1,0:T(8,128)(2,1)S(1)} %get-tuple-element.8.a_ref, bf16[64,4096]{1,0:T(8,128)(2,1)S(1)} %get-tuple-element.9.gq_ref, bf16[64,2048]{1,0:T(8,128)(2,1)S(1)} %get-tuple-element.10.gk_ref, ...), custom_call_target="tpu_custom_call" | custom-call | tf_op jit(solution)/shard_map/pallas_call | solution.py:417

commit v6 on v5

--- a/solution.py
+++ b/solution.py
@@ -60,9 +60,9 @@
         return ((z * 4 + core * 2 + yy) * 2 + c, (x + dx) % 4)
 
     barrier = pltpu.get_barrier_semaphore()
-    for yy in range(2):
-        for c in range(2):
-            for dx in range(4):
+    for dx in (2, 1, 3, 0):
+        for yy in range(2):
+            for c in range(2):
                 pl.semaphore_signal(barrier, inc=1, device_id=source(yy, c, dx), device_id_type=MESH)
 
     @pl.when(has_before)
@@ -110,8 +110,10 @@
             pl.when(local)(lambda: pltpu.make_async_copy(src, dst, recv_sem).start())
             pl.when(jnp.logical_not(local))(far)
 
-    offsets = [(dx, dy) for dx in range(4) for dy in range(4)]
-    offsets = sorted(offsets, key=lambda o: -min(o[0], 4 - o[0]) - min(o[1], 4 - o[1]))
+    offsets = (
+        (2, 2), (2, 1), (1, 2), (2, 3), (3, 2), (1, 1), (3, 3), (1, 3),
+        (3, 1), (2, 0), (0, 2), (1, 0), (3, 0), (0, 1), (0, 3), (0, 0),
+    )
     own_rows = pl.ds(pl.multiple_of(slot * ROWS, ROWS), ROWS)
     own_rows2 = pl.ds(pl.multiple_of(WINDOW + slot * ROWS, ROWS), ROWS)
     loads[4].wait()

time: 45.6 us -> 45.9 us (level)
  no operation moved by 1% of the time
where the time goes in v6:
time: 45.9 us; the launch traced here: 45.4 us
  Pallas kernels  44.8 us (98%)
  between operations  0.64 us (1%)
    pallas_call x1, Pallas kernels, body(): pl.pallas_call(kernel, out_shape=outs, in_specs=[pl.BlockSpec(memory_spac...  43.6 us
    pallas_call x1, Pallas kernels, body(): pl.pallas_call(deliver, out_shape=outs, in_specs=[pl.BlockSpec(memory_spa...  1.17 us

profile of v6, /device:TPU:1, one launch (start us, length us, event | category | flops | bytes accessed | tf_op | source)
XLA Modules:
  0.0 45.4 jit_solution(10940112918821326831)
XLA Ops:
  0.6 43.6 %shard_map.84 = (bf16[64,4096]{1,0:T(8,128)(2,1)S(1)}, bf16[64,4096]{1,0:T(8,128)(2,1)S(1)}, bf16[64,2048]{1,0:T(8,128)(2,1)S(1)}, bf16[64,2048]{1,0:T(8,128)(2,1)S(1)}) custom-call(bf16[64,4096]{1,0:T(8,128)(2,1)} %q_ref.1, bf16[64,2048]{1,0:T(8,128)(2,1)} %k_ref.1, bf16[64,2048]{1,0:T(8,128)(2,1)} %v_ref.1, bf16[64,4096]{1,0:T(8,128)(2,1)} %g_ref.1, ...), custom_call_target="tpu_custom_call" | custom-call | tf_op jit(solution)/shard_map/pallas_call | solution.py:374
  44.3 1.2 %shard_map.85 = (bf16[64,4096]{1,0:T(8,128)(2,1)}, bf16[64,4096]{1,0:T(8,128)(2,1)}, bf16[64,2048]{1,0:T(8,128)(2,1)}, bf16[64,2048]{1,0:T(8,128)(2,1)}) custom-call(bf16[64,4096]{1,0:T(8,128)(2,1)S(1)} %get-tuple-element.8.a_ref, bf16[64,4096]{1,0:T(8,128)(2,1)S(1)} %get-tuple-element.9.gq_ref, bf16[64,2048]{1,0:T(8,128)(2,1)S(1)} %get-tuple-element.10.gk_ref, ...), custom_call_target="tpu_custom_call" | custom-call | tf_op jit(solution)/shard_map/pallas_call | solution.py:419
